TPU v7x, 16 devices: a 4x2x1 block of a 4x4x8 slice. The times are simulated.
16 devices in a mesh: dp: 2 (over y, z), stage: 8 (over x, core).
Axes of the slice: x: 4, y: 2, z: 1, core: 2. Of those that a mesh axis runs over, the one named last changes fastest.
The devices are a block of a 4x4x8 slice.
Arguments:
- token_ids: int32 [16, 256], P('dp'), parts along dimension 0
- label_ids: int32 [16, 256], P('dp'), parts along dimension 0
- label2_ids: int32 [16, 256], P('dp'), parts along dimension 0
- embed_table: bfloat16 [32128, 512], replicated
- w_up: bfloat16 [8, 512, 4096], P('stage')
- w_down: bfloat16 [8, 4096, 512], P('stage')
- mtp_up: bfloat16 [512, 4096], replicated
- mtp_down: bfloat16 [4096, 512], replicated
Outputs:
- output 1: float32 [2], P('dp'), parts along dimension 0
- output 2: float32 [16, 512, 4096], P(('dp', 'stage')), parts along dimension 0
- output 3: float32 [16, 4096, 512], P(('dp', 'stage')), parts along dimension 0
- output 4: float32 [64256, 512], P('dp'), parts along dimension 0
There are 2 independent parts. A program takes and returns all parts, laid end to end along the dimension named above; an argument that names none is the same for every part.
All inputs are finite; a program needn't handle non-finite values.
Results may differ from a plain program's by a relative error of at most 0.0140777.
Values are sent between devices in bfloat16 or wider.
A program may use at most 768 MiB of HBM per device.

v0:
```python
import jax
import jax.numpy as jnp
from jax import lax
from jax.sharding import PartitionSpec as P

EPS_NORM = 1e-6


def mlp_block(x_in, w_in, w_out):
    pre_act = jnp.dot(x_in, w_in, preferred_element_type=jnp.float32)
    hid_act = jax.nn.gelu(pre_act).astype(jnp.bfloat16)
    out_f = x_in.astype(jnp.float32) + jnp.dot(hid_act, w_out, preferred_element_type=jnp.float32)
    return out_f.astype(jnp.bfloat16)


def block_back(x_in, d_out, w_in, w_out):
    pre_act = jnp.dot(x_in, w_in, preferred_element_type=jnp.float32)
    gelu_out, gelu_back = jax.vjp(jax.nn.gelu, pre_act)
    hid_act = gelu_out.astype(jnp.bfloat16)
    d_hid = jnp.einsum('td,fd->tf', d_out, w_out, preferred_element_type=jnp.float32)
    d_pre = gelu_back(d_hid)[0].astype(jnp.bfloat16)
    d_in = d_out.astype(jnp.float32) + jnp.einsum('tf,df->td', d_pre, w_in, preferred_element_type=jnp.float32)
    return d_in, d_pre, hid_act


def rms_fwd(stacked):
    stack_f = stacked.astype(jnp.float32)
    inv_rms = lax.rsqrt(jnp.mean(stack_f * stack_f, axis=-1, keepdims=True) + EPS_NORM)
    return stack_f * inv_rms, inv_rms


def rms_back(normed_f, inv_rms, d_norm):
    return inv_rms * (d_norm - normed_f * jnp.mean(d_norm * normed_f, axis=-1, keepdims=True))


def heads_back(hidden, lab_m, lab2_m, embed_table, mtp_up, mtp_down):
    vocab_size, model_width = embed_table.shape
    logit_scale = model_width ** -0.5
    n_tok = hidden.shape[0]
    g_in = (hidden.astype(jnp.float32) + embed_table[lab_m].astype(jnp.float32)).astype(jnp.bfloat16)
    g_out = mlp_block(g_in, mtp_up, mtp_down)
    stacked = jnp.concatenate([hidden, g_out], axis=0)
    targets = jnp.concatenate([lab_m, lab2_m], axis=0)
    normed_f, inv_rms = rms_fwd(stacked)
    normed = normed_f.astype(jnp.bfloat16)
    logits = jnp.einsum('td,vd->tv', normed, embed_table, preferred_element_type=jnp.float32) * logit_scale
    log_norm = jax.nn.logsumexp(logits, axis=-1)
    is_label = targets[:, None] == lax.broadcasted_iota(jnp.int32, (1, vocab_size), 1)
    picked = jnp.sum(jnp.where(is_label, logits, 0.0), axis=-1)
    soft_probs = jnp.exp(logits - log_norm[:, None])
    d_logit = (0.5 * logit_scale * (soft_probs - is_label.astype(jnp.float32))).astype(jnp.bfloat16)
    head_grad = jnp.einsum('tv,td->vd', d_logit, normed, preferred_element_type=jnp.float32)
    d_norm = jnp.dot(d_logit, embed_table, preferred_element_type=jnp.float32)
    d_stack = rms_back(normed_f, inv_rms, d_norm)
    d_gin, _, _ = block_back(g_in, d_stack[n_tok:].astype(jnp.bfloat16), mtp_up, mtp_down)
    emb_grad = head_grad + jax.ops.segment_sum(d_gin, lab_m, num_segments=vocab_size)
    d_hidden = (d_stack[:n_tok] + d_gin).astype(jnp.bfloat16)
    return 0.5 * jnp.sum(log_norm - picked), emb_grad, d_hidden


def solution(mesh):
    n_stage = mesh.shape['stage']
    fwd_perm = [(i, i + 1) for i in range(n_stage - 1)]
    bwd_perm = [(i + 1, i) for i in range(n_stage - 1)]

    def per_device(token_ids, label_ids, label2_ids, embed_table, w_up, w_down, mtp_up, mtp_down):
        n_micro, n_tok = token_ids.shape
        vocab_size, model_width = embed_table.shape
        stage_id = lax.axis_index('stage')
        is_first = stage_id == 0
        is_last = stage_id == n_stage - 1
        w_in = w_up[0]
        w_out = w_down[0]
        n_steps = n_micro + n_stage - 1
        act_store = jnp.zeros((n_micro, n_tok, model_width), jnp.bfloat16)
        zero_act = jnp.zeros((n_tok, model_width), jnp.bfloat16)

        def fwd_step(loop_state, step_idx):
            incoming, saved_in, saved_out = loop_state
            micro_id = step_idx - stage_id
            is_valid = (micro_id >= 0) & (micro_id < n_micro)
            mb_slot = jnp.clip(micro_id, 0, n_micro - 1)
            tok_row = lax.dynamic_index_in_dim(token_ids, mb_slot, 0, keepdims=False)
            x_in = lax.cond(is_first, lambda: embed_table[tok_row], lambda: incoming)
            x_out = lax.cond(is_valid, lambda: mlp_block(x_in, w_in, w_out), lambda: x_in)
            old_in = lax.dynamic_index_in_dim(saved_in, mb_slot, 0, keepdims=False)
            saved_in = lax.dynamic_update_index_in_dim(saved_in, jnp.where(is_valid, x_in, old_in), mb_slot, 0)
            old_out = lax.dynamic_index_in_dim(saved_out, mb_slot, 0, keepdims=False)
            saved_out = lax.dynamic_update_index_in_dim(saved_out, jnp.where(is_valid, x_out, old_out), mb_slot, 0)
            sent_act = lax.ppermute(x_out, 'stage', fwd_perm)
            return (sent_act, saved_in, saved_out), None

        (_, saved_in, saved_out), _ = lax.scan(fwd_step, (zero_act, act_store, act_store), jnp.arange(n_steps))

        def head_phase(hidden_all):
            def head_step(loop_state, packed):
                loss_acc, grad_acc = loop_state
                hidden, lab_m, lab2_m = packed
                loss_m, grad_m, d_hidden = heads_back(hidden, lab_m, lab2_m, embed_table, mtp_up, mtp_down)
                return (loss_acc + loss_m, grad_acc + grad_m), d_hidden
            init_state = (jnp.zeros((), jnp.float32), jnp.zeros((vocab_size, model_width), jnp.float32))
            (loss_sum, grad_sum), d_hidden_all = lax.scan(head_step, init_state, (hidden_all, label_ids, label2_ids))
            return loss_sum, grad_sum, d_hidden_all

        def head_skip(hidden_all):
            return jnp.zeros((), jnp.float32), jnp.zeros((vocab_size, model_width), jnp.float32), jnp.zeros_like(hidden_all)

        loss_sum, head_part, d_hidden_all = lax.cond(is_last, head_phase, head_skip, saved_out)

        def bwd_step(loop_state, step_idx):
            incoming, up_acc, down_acc, saved_dx = loop_state
            micro_id = step_idx - (n_stage - 1 - stage_id)
            is_valid = (micro_id >= 0) & (micro_id < n_micro)
            mb_slot = jnp.clip(micro_id, 0, n_micro - 1)
            d_out = lax.cond(is_last, lambda: lax.dynamic_index_in_dim(d_hidden_all, mb_slot, 0, keepdims=False), lambda: incoming)
            x_in = lax.dynamic_index_in_dim(saved_in, mb_slot, 0, keepdims=False)

            def run_back():
                d_in, d_pre, hid_act = block_back(x_in, d_out, w_in, w_out)
                return (d_in.astype(jnp.bfloat16), jnp.einsum('td,tf->df', x_in, d_pre, preferred_element_type=jnp.float32), jnp.einsum('tf,td->fd', hid_act, d_out, preferred_element_type=jnp.float32))

            def skip_back():
                return d_out, jnp.zeros_like(up_acc), jnp.zeros_like(down_acc)

            d_send, g_up, g_down = lax.cond(is_valid, run_back, skip_back)
            old_dx = lax.dynamic_index_in_dim(saved_dx, mb_slot, 0, keepdims=False)
            saved_dx = lax.dynamic_update_index_in_dim(saved_dx, jnp.where(is_valid, d_send, old_dx), mb_slot, 0)
            sent_grad = lax.ppermute(d_send, 'stage', bwd_perm)
            return (sent_grad, up_acc + g_up, down_acc + g_down, saved_dx), None

        init_back = (zero_act, jnp.zeros(w_in.shape, jnp.float32), jnp.zeros(w_out.shape, jnp.float32), act_store)
        (_, up_sum, down_sum, saved_dx), _ = lax.scan(bwd_step, init_back, jnp.arange(n_steps))

        def embed_grad(dx_rows):
            return jax.ops.segment_sum(dx_rows.reshape(-1, model_width).astype(jnp.float32), token_ids.reshape(-1), num_segments=vocab_size)

        def embed_skip(dx_rows):
            return jnp.zeros((vocab_size, model_width), jnp.float32)

        local_grad = head_part + lax.cond(is_first, embed_grad, embed_skip, saved_dx)
        grad_all = lax.psum(local_grad, 'stage')
        mean_loss = (lax.psum(loss_sum, 'stage') / (n_micro * n_tok)).reshape(1)
        return mean_loss, up_sum[None], down_sum[None], grad_all

    in_specs = (P('dp', None), P('dp', None), P('dp', None), P(None, None), P('stage', None, None), P('stage', None, None), P(None, None), P(None, None))
    out_specs = (P('dp'), P(('dp', 'stage'), None, None), P(('dp', 'stage'), None, None), P('dp', None))
    return jax.shard_map(per_device, mesh=mesh, in_specs=in_specs, out_specs=out_specs, check_vma=False)
```

profile of v0, /device:TPU:112, one launch (start us, length us, event | category | flops | bytes accessed | tf_op | source)
XLA Modules:
  0.0 3647.5 jit_solution(14223030686112754773)
XLA Ops:
  9.0 190.1 %while.55 = (s32[]{:T(128)}, bf16[256,512]{1,0:T(8,128)(2,1)S(1)}, bf16[8,256,512]{2,1,0:T(8,128)(2,1)S(1)}, bf16[8,256,512]{2,1,0:T(8,128)(2,1)}, s32[15]{0:T(1...) while((s32[]{:T(128)}, bf16[256,512]{1,0:T(8,128)(2,1)S(1)}, ...), condition=%wide.region_5.6_spmd, body=%wide.region_0.5_spmd.sunk | while | flops 2157577984 | bytes 13642577 | solution.py:93
  13.8 6.1 conditional.15
  42.0 6.1 conditional.15
  56.1 6.1 conditional.15
  70.2 6.1 conditional.15
  98.4 6.1 conditional.15
  127.0 8.4 collective-permute-start
  151.2 8.4 collective-permute-start
  200.5 22.8 conditional.6
  200.5 21.3 broadcast.171
  223.5 2405.2 %while.56 = (s32[]{:T(128)}, bf16[256,512]{1,0:T(8,128)(2,1)S(1)}, f32[512,4096]{1,0:T(8,128)}, f32[4096,512]{1,0:T(8,128)}, bf16[8,256,512]{2,1,0:T(8,128)(2,1)...) while((s32[]{:T(128)}, bf16[256,512]{1,0:T(8,128)(2,1)S(1)}, ...), condition=%wide.region_23.24_spmd.clone, body=%wide.region_18.23_spmd.clone.sunk | while | flops 5408030720 | bytes 123995584 | solution.py:132
  224.8 8.6 conditional.17
  234.7 9.2 select_add_fusion.4
  243.9 8.9 select_add_fusion.5
  254.2 8.6 conditional.17
  264.1 11.6 select_add_fusion.4
  275.6 11.3 select_add_fusion.5
  288.3 8.6 conditional.17
  298.2 11.6 select_add_fusion.4
  309.8 11.3 select_add_fusion.5
  322.5 8.6 conditional.17
  332.4 11.6 select_add_fusion.4
  343.9 11.3 select_add_fusion.5
  356.6 8.6 conditional.17
  366.5 11.6 select_add_fusion.4
  378.1 11.3 select_add_fusion.5
  390.8 8.6 conditional.17
  400.6 11.6 select_add_fusion.4
  412.2 11.3 select_add_fusion.5
  424.9 8.6 conditional.17
  434.8 11.6 select_add_fusion.4
  446.4 11.3 select_add_fusion.5
  457.7 1803.2 %collective-permute-done.1 = bf16[256,512]{1,0:T(8,128)(2,1)S(1)} collective-permute-done((bf16[256,512]{1,0:T(8,128)(2,1)S(1)}, bf16[256,512]{1,0:T(8,128)(2,1)S(1)}, u32[]{:S(2)}, u32[]{:S(2)}) %collective-permute-start.1) | collective-permute-done | bytes 262176 | tf_op jit(solution)/shard_map/while/body/eval_jaxpr/ppermute | solution.py:128
  2262.2 19.8 conditional.17
  2283.3 11.6 select_add_fusion.4
  2294.9 11.3 select_add_fusion.5
  2308.2 19.8 conditional.17
  2329.4 11.6 select_add_fusion.4
  2340.9 11.3 select_add_fusion.5
  2354.3 19.8 conditional.17
  2375.4 11.6 select_add_fusion.4
  2387.0 11.3 select_add_fusion.5
  2400.3 19.8 conditional.17
  2421.4 11.6 select_add_fusion.4
  2433.0 11.3 select_add_fusion.5
  2446.3 19.8 conditional.17
  2467.5 11.6 select_add_fusion.4
  2479.0 11.3 select_add_fusion.5
  2492.4 19.8 conditional.17
  2513.5 11.6 select_add_fusion.4
  2525.1 11.3 select_add_fusion.5
  2538.4 19.8 conditional.17
  2559.5 11.6 select_add_fusion.4
  2571.1 11.3 select_add_fusion.5
  2584.4 19.8 conditional.17
  2605.5 11.6 select_add_fusion.4
  2617.1 11.3 select_add_fusion.5
  2628.7 270.1 %conditional.7 = (f32[32128,512]{1,0:T(8,128)}) conditional(s32[]{:T(128)} %convert_element_type.136, () %tuple.83, (s32[8,256]{1,0:T(8,128)S(1)}, bf16[8,256,512]{2,1,0:T(8,128)(2,1)S(1)}) %tuple.175), branch_computations={%region_24.25_spmd, %region_25.27_spmd} | conditional | flops 2097152 | bytes 84697096 | solution.py:140
  2631.4 21.0 broadcast.195
  2652.5 246.4 %scatter_fusion = f32[32128,512]{1,0:T(8,128)} fusion(f32[32128,512]{1,0:T(8,128)} %broadcast.195, s32[2048]{0:T(1024)S(1)} %bitcast.119, f32[2048,512]{1,0:T(8,128)} %bitcast_convert_fusion), kind=kCustom, calls=%fused_computation.3 | custom fusion | flops 1048576 | bytes 12591104 | tf_op jit(solution)/shard_map/cond/branch_1_fun/scatter-add | solution.py:135
  2898.8 63.1 %add.165 = f32[32128,512]{1,0:T(8,128)} add(f32[32128,512]{1,0:T(8,128)} %get-tuple-element.432, f32[32128,512]{1,0:T(8,128)} %get-tuple-element.956) | non-fusion elementwise | flops 16449536 | bytes 197394432 | tf_op jit(solution)/shard_map/add | solution.py:140
  2962.0 13.7 psum.14
  2976.4 620.1 %all-reduce.2.cloned.1.call-done = f32[32128,512]{1,0:T(8,128)} async-done(((f32[32128,512]{1,0:T(8,128)}), f32[32128,512]{1,0:T(8,128)}) %all-reduce.2.cloned.1.call-update) | async-done | bytes 65798160 | tf_op jit(solution)/shard_map/psum | solution.py:141
  3596.4 43.1 %copy.94 = f32[32128,512]{1,0:T(8,128)} copy(f32[32128,512]{1,0:T(8,128)} %all-reduce.2.cloned.1.call-done) | data formatting | bytes 131596288
  (387 shorter events, 494.6 us)
Async XLA Ops:
  7.2 3589.3 %all-reduce.2.cloned.1.call-start = ((), (), s32[]{:S(2)}) async-start(), calls=%async_computation | async-start | bytes 131596288 | tf_op jit(solution)/shard_map/psum | solution.py:141
  19.9 3.2 collective-permute-start
  34.0 3.2 collective-permute-start
  48.1 3.2 collective-permute-start
  62.2 3.2 collective-permute-start
  76.3 3.2 collective-permute-start
  90.5 3.2 collective-permute-start
  104.6 3.2 collective-permute-start
  118.7 3.5 collective-permute-start
  127.0 10.3 collective-permute-start
  142.1 4.2 collective-permute-start
  151.2 10.3 collective-permute-start
  166.3 4.2 collective-permute-start
  175.4 4.2 collective-permute-start
  184.4 4.2 collective-permute-start
  193.5 5.7 collective-permute-start
  199.1 1.3 copy-start.1
  223.5 2405.2 %copy-start.4 = (s32[8,256]{1,0:T(8,128)S(1)}, s32[8,256]{1,0:T(8,128)}, u32[]{:S(2)}) copy-start(s32[8,256]{1,0:T(8,128)} %get-tuple-element.970) | copy-start | bytes 24580
  233.4 19.5 collective-permute-start.1
  262.8 24.3 collective-permute-start.1
  296.9 24.3 collective-permute-start.1
  331.0 24.3 collective-permute-start.1
  365.2 24.3 collective-permute-start.1
  399.3 24.3 collective-permute-start.1
  433.5 1827.4 %collective-permute-start.1 = (bf16[256,512]{1,0:T(8,128)(2,1)S(1)}, bf16[256,512]{1,0:T(8,128)(2,1)S(1)}, u32[]{:S(2)}, u32[]{:S(2)}) collective-permute-start(bf16[256,512]{1,0:T(8,128)(2,1)S(1)} %get-tuple-element.786), channel_id=1, source_target_pairs={{1,0},{2,1},{3,2},{4,3},{5,4},{6,5},{7,6},{9,8},{10,9},{11,10},{12... | collective-permute-start | bytes 786440 | tf_op jit(solution)/shard_map/while/body/eval_jaxpr/ppermute | solution.py:128
  2262.2 3.6 copy-start.6
  2282.0 24.9 collective-permute-start.1
  2308.3 3.6 copy-start.6
  2328.1 24.9 collective-permute-start.1
  2354.3 3.6 copy-start.6
  2374.1 24.9 collective-permute-start.1
  2400.3 3.6 copy-start.6
  2420.1 24.9 collective-permute-start.1
  2446.3 3.6 copy-start.6
  2466.2 24.9 collective-permute-start.1
  2492.4 3.6 copy-start.6
  2512.2 24.9 collective-permute-start.1
  2538.4 3.6 copy-start.6
  2558.2 24.9 collective-permute-start.1
  2584.4 3.6 copy-start.6
  2604.2 24.3 collective-permute-start.1
Sparse Core Ops, SparseCore 0:
  2962.1 634.3 all-reduce.1
where the time goes:
time: 3670 us; the launch traced here: 3650 us
  waiting for transfers between devices  2430 us (66%)
  other arithmetic  664 us (18%)
  local copies, waits for them, and re-layouts  236 us (6%)
  matrix products  207 us (6%)
  starting transfers between devices  60.4 us (2%)
    ppermute x15, waiting for transfers between devices, bwd_step(): sent_grad = lax.ppermute(d_send, 'stage', bwd_perm)  1810 us
    psum x1, waiting for transfers between devices, per_device(): grad_all = lax.psum(local_grad, 'stage')  620 us
    add x30, other arithmetic, bwd_step(): return ((sent_grad, up_acc + g_up, down_acc + g_down, saved_dx), None)  338 us
    scatter-add x1, other arithmetic, embed_grad(): jax.ops.segment_sum(dx_rows.reshape(-1, model_width).astype(jnp.float32),...  246 us
    another operation x35, local copies, waits for them, and re-layouts  106 us
  transfers between devices with their start and end apart: 31, of which 9 were waited for; matrix products, arithmetic and copies ran while one was open for 10% of the time, Pallas kernels for 0%

commit v1 on v0

v1 whole, which is shorter than its diff:
```python
import functools
import math

import jax
import jax.numpy as jnp
from jax import lax
from jax.experimental import pallas as pl
from jax.experimental.pallas import tpu as pltpu
from jax.sharding import PartitionSpec as P

EPS_NORM = 1e-6
BF = jnp.bfloat16
F32 = jnp.float32
AXIS = 'stage'
GELU_A = math.sqrt(2.0 / math.pi)
GELU_B = 0.044715
VMEM_MAX = 67000000

VMEM = pl.BlockSpec(memory_space=pltpu.VMEM)
ANY = pl.BlockSpec(memory_space=pl.ANY)
SMEM = pl.BlockSpec(memory_space=pltpu.SMEM)
NN = (((1,), (0,)), ((), ()))
NT = (((1,), (1,)), ((), ()))


def mm(a, b):
    return lax.dot_general(a, b, NN, preferred_element_type=F32)


def mm_t(a, b):
    return lax.dot_general(a, b, NT, preferred_element_type=F32)


def gelu(v):
    return 0.5 * v * (1.0 + jnp.tanh(GELU_A * (v + GELU_B * (v * v * v))))


def gelu_both(v):
    sq = v * v
    t = jnp.tanh(GELU_A * (v + GELU_B * (sq * v)))
    half = 0.5 * (1.0 + t)
    slope = half + (0.5 * v) * (1.0 - t * t) * (GELU_A * (1.0 + (3.0 * GELU_B) * sq))
    return v * half, slope


def dev(d):
    return {AXIS: d}


def greet_all(n_dev):
    me = lax.axis_index(AXIS)
    bar = pltpu.get_barrier_semaphore()
    for d in range(1, n_dev):
        pl.semaphore_signal(bar, inc=1, device_id=dev(lax.rem(me + d, n_dev)), device_id_type=pl.DeviceIdType.MESH)
    pl.semaphore_wait(bar, n_dev - 1)
    return me


def rcopy(src, dst, ssem, rsem, d):
    return pltpu.make_async_remote_copy(src_ref=src, dst_ref=dst, send_sem=ssem, recv_sem=rsem, device_id=dev(d), device_id_type=pl.DeviceIdType.MESH)


def rows(c, size):
    return pl.ds(pl.multiple_of(c * size, size), size)


def mlp_rows(x, wi_ref, wo_ref, tile):
    acc = None
    for f in range(0, wi_ref.shape[1], tile):
        hid = gelu(mm(x, wi_ref[:, f:f + tile])).astype(BF)
        part = mm(hid, wo_ref[f:f + tile, :])
        acc = part if acc is None else acc + part
    return (x.astype(F32) + acc).astype(BF)


def fwd_kernel(S, C, tile, x_ref, wi_ref, wo_ref, xs_ref, h_ref, ob, own_sem, send_sem, recv_sem, h_sem):
    n_rows = xs_ref.shape[0]
    own = x_ref.shape[0]
    n_chunk, per = n_rows // C, own // C
    me = greet_all(S)
    nxt = lax.rem(me + 1, S)

    def own_copy(j):
        c = me * per + j
        return rcopy(x_ref.at[rows(j, C)], xs_ref.at[rows(c, C)], own_sem.at[j], recv_sem.at[c], lax.rem(S - me, S))

    @pl.when(me > 0)
    def _():
        for j in range(per):
            rcopy(x_ref.at[rows(j, C)], xs_ref.at[rows(me * per + j, C)], own_sem.at[j], recv_sem.at[me * per + j], 0).start()

    @pl.when(me == 0)
    def _():
        xs_ref[0:own, :] = x_ref[...]

    def step(c, carry):
        @pl.when((me > 0) | (c >= per))
        def _():
            rcopy(xs_ref.at[rows(c, C)], xs_ref.at[rows(c, C)], send_sem.at[c], recv_sem.at[c], nxt).wait_recv()

        ob[rows(c, C), :] = mlp_rows(xs_ref[rows(c, C), :], wi_ref, wo_ref, tile)
        owner = c // per
        j = lax.rem(c, per)

        @pl.when(me < S - 1)
        def _():
            rcopy(ob.at[rows(c, C)], xs_ref.at[rows(c, C)], send_sem.at[c], recv_sem.at[c], nxt).start()

        @pl.when((me == S - 1) & (owner < S - 1))
        def _():
            rcopy(ob.at[rows(c, C)], h_ref.at[rows(j, C)], send_sem.at[c], h_sem.at[j], owner).start()

        @pl.when((me == S - 1) & (owner == S - 1))
        def _():
            h_ref[rows(j, C), :] = ob[rows(c, C), :]
        return carry

    lax.fori_loop(0, n_chunk, step, 0)

    @pl.when(me > 0)
    def _():
        for j in range(per):
            rcopy(x_ref.at[rows(j, C)], xs_ref.at[rows(me * per + j, C)], own_sem.at[j], recv_sem.at[me * per + j], 0).wait_send()

    def drain(c, carry):
        @pl.when((me < S - 1) | (c < (S - 1) * per))
        def _():
            rcopy(ob.at[rows(c, C)], xs_ref.at[rows(c, C)], send_sem.at[c], recv_sem.at[c], nxt).wait_send()
        return carry

    lax.fori_loop(0, n_chunk, drain, 0)

    @pl.when(me < S - 1)
    def _():
        for j in range(per):
            rcopy(ob.at[rows(j, C)], h_ref.at[rows(j, C)], send_sem.at[j], h_sem.at[j], nxt).wait_recv()


def forward(S, C, tile, x_own, w_in, w_out):
    own, width = x_own.shape
    n_rows = own * S
    n_chunk, per = n_rows // C, own // C
    return pl.pallas_call(
        functools.partial(fwd_kernel, S, C, tile),
        out_shape=(jax.ShapeDtypeStruct((n_rows, width), BF), jax.ShapeDtypeStruct((own, width), BF)),
        in_specs=[VMEM] * 3,
        out_specs=(VMEM, VMEM),
        scratch_shapes=[
            pltpu.VMEM((n_rows, width), BF),
            pltpu.SemaphoreType.DMA((per,)),
            pltpu.SemaphoreType.DMA((n_chunk,)),
            pltpu.SemaphoreType.DMA((n_chunk,)),
            pltpu.SemaphoreType.DMA((per,)),
        ],
        compiler_params=pltpu.CompilerParams(collective_id=0, has_side_effects=True, vmem_limit_bytes=VMEM_MAX),
        cost_estimate=pl.CostEstimate(flops=4 * n_rows * width * w_in.shape[1], bytes_accessed=4 * w_in.size, transcendentals=0),
        name='fwd_pipe',
    )(x_own, w_in, w_out)


def heads_kernel(S, TV, tile, h_ref, e1_ref, e2_ref, tg_ref, wi_ref, wo_ref, emb_ref,
                 nall_ref, lall_ref, dh_ref, dg_ref,
                 ebuf, erem, lrow, gbuf, nf_buf, inv_buf, dn_buf, esem, rsem, nsend, nrecv, lsend, lrecv):
    R, D = h_ref.shape
    V = emb_ref.shape[0]
    n_full = V // TV
    rem = V - n_full * TV
    scale = D ** -0.5
    c2 = scale * math.log2(math.e)
    k = 0.5 * scale
    me = greet_all(S)

    def fetch(i, slot):
        return pltpu.make_async_copy(emb_ref.at[rows(i, TV)], ebuf.at[slot], esem.at[slot])

    fetch(0, 0).start()
    rem_copy = pltpu.make_async_copy(emb_ref.at[pl.ds(n_full * TV, rem)], erem, rsem)
    rem_copy.start()

    hf = h_ref[...].astype(F32)
    g_in = (hf + e1_ref[...].astype(F32)).astype(BF)
    gbuf[...] = g_in
    g_out = mlp_rows(g_in, wi_ref, wo_ref, tile).astype(F32)
    for j, v in enumerate((hf, g_out)):
        inv = lax.rsqrt(jnp.mean(v * v, axis=-1, keepdims=True) + EPS_NORM)
        nf = v * inv
        nf_buf[j * R:(j + 1) * R, :] = nf
        inv_buf[j * R:(j + 1) * R, :] = jnp.broadcast_to(inv, (R, 128))
        nall_ref[me, j * R:(j + 1) * R, :] = nf.astype(BF)

    def ncopy(d):
        return rcopy(nall_ref.at[me], nall_ref.at[me], nsend.at[d], nrecv.at[d], lax.rem(me + d, S))

    def lcopy(d):
        return rcopy(lall_ref.at[me], lall_ref.at[me], lsend.at[d], lrecv.at[d], lax.rem(me + d, S))

    for d in range(1, S):
        ncopy(d).start()

    def fold(et, mx, sm):
        lt = mm_t(et, nall_ref[me])
        grp = lt.reshape(et.shape[0] // 8, 8, 2 * R)
        new = jnp.maximum(mx, jnp.max(grp, axis=0))
        sm = sm * jnp.exp2((mx - new) * c2) + jnp.sum(jnp.exp2((grp - new[None]) * c2), axis=0)
        return new, sm

    def p1(i, carry):
        slot = lax.rem(i, 2)
        fetch(i, slot).wait()

        fetch(lax.rem(i + 1, n_full), 1 - slot).start()
        return fold(ebuf[slot], *carry)

    mx, sm = lax.fori_loop(0, n_full, p1, (jnp.full((8, 2 * R), -jnp.inf, F32), jnp.zeros((8, 2 * R), F32)))
    rem_copy.wait()
    mx, sm = fold(erem[...], mx, sm)
    top = jnp.max(mx, axis=0, keepdims=True)
    tot = jnp.sum(sm * jnp.exp2((mx - top) * c2), axis=0, keepdims=True)
    lse2 = top * c2 + jnp.log(tot) * math.log2(math.e)
    lrow[...] = jnp.broadcast_to(lse2, (128, 2 * R))
    lcol = jnp.transpose(lrow[...])[:, 0:1]
    nrm = nall_ref[me].astype(F32)
    pick = jnp.concatenate([
        jnp.sum(nrm[:R] * e1_ref[...].astype(F32), axis=-1, keepdims=True),
        jnp.sum(nrm[R:] * e2_ref[...].astype(F32), axis=-1, keepdims=True)], axis=0) * scale
    nll = jnp.sum(lcol * math.log(2.0) - pick, axis=0, keepdims=True)
    lall_ref[me] = jnp.where(lax.broadcasted_iota(jnp.int32, (8, 2 * R), 0) == 0, jnp.broadcast_to(lse2, (8, 2 * R)), jnp.broadcast_to(nll, (8, 2 * R)))
    for d in range(1, S):
        lcopy(d).start()

    shift = lcol - math.log2(k)
    tg = tg_ref[...]
    dn_buf[...] = jnp.zeros_like(dn_buf)

    def back(et, base):
        n = et.shape[0]
        logit = mm_t(nall_ref[me], et)
        q = jnp.exp2(logit * c2 - shift)
        hit = lax.broadcasted_iota(jnp.int32, (2 * R, n), 1) == tg - base
        dl = jnp.where(hit, q - k, q).astype(BF)
        dn_buf[...] += mm(dl, et)

    first = n_full % 2

    def p2(i, carry):
        slot = lax.rem(i + first, 2)
        fetch(i, slot).wait()

        @pl.when(i + 1 < n_full)
        def _():
            fetch(i + 1, 1 - slot).start()
        back(ebuf[slot], i * TV)
        return carry

    lax.fori_loop(0, n_full, p2, 0)
    back(erem[...], n_full * TV)

    dn = dn_buf[...]
    nf = nf_buf[...]
    ds = inv_buf[:, 0:1] * (dn - nf * jnp.mean(dn * nf, axis=-1, keepdims=True))
    dout = ds[R:].astype(BF)
    g_in = gbuf[...]
    acc = dout.astype(F32)
    for f in range(0, wi_ref.shape[1], tile):
        w1 = wi_ref[:, f:f + tile]
        _, slope = gelu_both(mm(g_in, w1))
        dpre = (mm_t(dout, wo_ref[f:f + tile, :]) * slope).astype(BF)
        acc += mm_t(dpre, w1)
    dg_ref[...] = acc
    dh_ref[...] = (ds[:R] + acc).astype(BF)

    for d in range(1, S):
        ncopy(d).wait_send()
        lcopy(d).wait_send()
        rcopy(nall_ref.at[me], nall_ref.at[lax.rem(me + S - d, S)], nsend.at[d], nrecv.at[d], lax.rem(me + d, S)).wait_recv()
        rcopy(lall_ref.at[me], lall_ref.at[lax.rem(me + S - d, S)], lsend.at[d], lrecv.at[d], lax.rem(me + d, S)).wait_recv()


def heads(S, TV, tile, h_own, e1, e2, tg, mtp_up, mtp_down, emb):
    R, D = h_own.shape
    V = emb.shape[0]
    rem = V % TV
    return pl.pallas_call(
        functools.partial(heads_kernel, S, TV, tile),
        out_shape=(jax.ShapeDtypeStruct((S, 2 * R, D), BF), jax.ShapeDtypeStruct((S, 8, 2 * R), F32),
                   jax.ShapeDtypeStruct((R, D), BF), jax.ShapeDtypeStruct((R, D), F32)),
        in_specs=[VMEM] * 6 + [ANY],
        out_specs=(VMEM,) * 4,
        scratch_shapes=[
            pltpu.VMEM((2, TV, D), BF),
            pltpu.VMEM((rem, D), BF),
            pltpu.VMEM((128, 2 * R), F32),
            pltpu.VMEM((R, D), BF),
            pltpu.VMEM((2 * R, D), F32),
            pltpu.VMEM((2 * R, 128), F32),
            pltpu.VMEM((2 * R, D), F32),
            pltpu.SemaphoreType.DMA((2,)),
            pltpu.SemaphoreType.DMA,
            pltpu.SemaphoreType.DMA((S,)),
            pltpu.SemaphoreType.DMA((S,)),
            pltpu.SemaphoreType.DMA((S,)),
            pltpu.SemaphoreType.DMA((S,)),
        ],
        compiler_params=pltpu.CompilerParams(collective_id=1, has_side_effects=True, vmem_limit_bytes=VMEM_MAX),
        cost_estimate=pl.CostEstimate(flops=12 * R * D * V, bytes_accessed=4 * V * D, transcendentals=4 * R * V),
        name='heads',
    )(h_own, e1, e2, tg, mtp_up, mtp_down, emb)


def bwd_kernel(S, C, tile, dh_ref, xs_ref, wi_ref, wo_ref, ds_ref, dpre_ref, hid_ref, dx_ref,
               ob, pbuf, hbuf, own_sem, send_sem, recv_sem, psem, hsem, bsend, brecv):
    n_rows = xs_ref.shape[0]
    own = dh_ref.shape[0]
    F = wi_ref.shape[1]
    n_chunk, per = n_rows // C, own // C
    me = greet_all(S)
    last = S - 1
    prv = lax.rem(me + S - 1, S)
    half = S // 2

    @pl.when(me < last)
    def _():
        for j in range(per):
            rcopy(dh_ref.at[rows(j, C)], ds_ref.at[rows(me * per + j, C)], own_sem.at[j], recv_sem.at[me * per + j], last).start()

    @pl.when(me == last)
    def _():
        ds_ref[last * own:, :] = dh_ref[...]

    def spread(c, stop):
        def to(i, d):
            cp = rcopy(dx_ref.at[rows(c, C)], dx_ref.at[rows(c, C)], bsend.at[i, c], brecv.at[c], d)
            cp.wait_send() if stop else cp.start()

        @pl.when(lax.rem(me, 2) == 0)
        def _():
            to(0, me + 1)

        @pl.when((lax.rem(me, 2) == 0) & (me < half))
        def _():
            to(1, me + 2)

        @pl.when((me == 0) | ((lax.rem(me, 2) == 0) & (me > half + 2)))
        def _():
            to(2, lax.rem(me + S - 2, S))

    def out_copies(c):
        slot = lax.rem(c, 2)
        return (pltpu.make_async_copy(pbuf.at[slot], dpre_ref.at[rows(c, C)], psem.at[slot]),
                pltpu.make_async_copy(hbuf.at[slot], hid_ref.at[rows(c, C)], hsem.at[slot]))

    def step(c, carry):
        slot = lax.rem(c, 2)

        @pl.when(c >= 2)
        def _():
            for cp in out_copies(c - 2):
                cp.wait()

        @pl.when((me < last) | (c < last * per))
        def _():
            rcopy(ds_ref.at[rows(c, C)], ds_ref.at[rows(c, C)], send_sem.at[c], recv_sem.at[c], prv).wait_recv()

        x = xs_ref[rows(c, C), :]
        dout = ds_ref[rows(c, C), :]
        acc = dout.astype(F32)
        for f in range(0, F, tile):
            w1 = wi_ref[:, f:f + tile]
            hid, slope = gelu_both(mm(x, w1))
            dpre = (mm_t(dout, wo_ref[f:f + tile, :]) * slope).astype(BF)
            hbuf[slot, :, f:f + tile] = hid.astype(BF)
            pbuf[slot, :, f:f + tile] = dpre
            acc += mm_t(dpre, w1)
        res = acc.astype(BF)

        @pl.when(me > 0)
        def _():
            ob[rows(c, C), :] = res
            rcopy(ob.at[rows(c, C)], ds_ref.at[rows(c, C)], send_sem.at[c], recv_sem.at[c], prv).start()

        @pl.when(me == 0)
        def _():
            dx_ref[rows(c, C), :] = res
            spread(c, False)

        for cp in out_copies(c):
            cp.start()
        return carry

    lax.fori_loop(0, n_chunk, step, 0)

    for c in (n_chunk - 2, n_chunk - 1):
        for cp in out_copies(c):
            cp.wait()

    @pl.when(me < last)
    def _():
        for j in range(per):
            rcopy(dh_ref.at[rows(j, C)], ds_ref.at[rows(me * per + j, C)], own_sem.at[j], recv_sem.at[me * per + j], last).wait_send()

    def drain(c, carry):
        @pl.when(me > 0)
        def _():
            rcopy(ob.at[rows(c, C)], ds_ref.at[rows(c, C)], send_sem.at[c], recv_sem.at[c], prv).wait_send()
            rcopy(dx_ref.at[rows(c, C)], dx_ref.at[rows(c, C)], bsend.at[0, c], brecv.at[c], prv).wait_recv()
            spread(c, False)
        return carry

    lax.fori_loop(0, n_chunk, drain, 0)

    def settle(c, carry):
        spread(c, True)
        return carry

    lax.fori_loop(0, n_chunk, settle, 0)


def backward(S, C, tile, dh, xs, w_in, w_out):
    own, D = dh.shape
    n_rows = xs.shape[0]
    F = w_in.shape[1]
    n_chunk, per = n_rows // C, own // C
    return pl.pallas_call(
        functools.partial(bwd_kernel, S, C, tile),
        out_shape=(jax.ShapeDtypeStruct((n_rows, D), BF), jax.ShapeDtypeStruct((n_rows, F), BF),
                   jax.ShapeDtypeStruct((n_rows, F), BF), jax.ShapeDtypeStruct((n_rows, D), BF)),
        in_specs=[VMEM] * 4,
        out_specs=(VMEM, ANY, ANY, VMEM),
        scratch_shapes=[
            pltpu.VMEM((n_rows, D), BF),
            pltpu.VMEM((2, C, F), BF),
            pltpu.VMEM((2, C, F), BF),
            pltpu.SemaphoreType.DMA((per,)),
            pltpu.SemaphoreType.DMA((n_chunk,)),
            pltpu.SemaphoreType.DMA((n_chunk,)),
            pltpu.SemaphoreType.DMA((2,)),
            pltpu.SemaphoreType.DMA((2,)),
            pltpu.SemaphoreType.DMA((3, n_chunk)),
            pltpu.SemaphoreType.DMA((n_chunk,)),
        ],
        compiler_params=pltpu.CompilerParams(collective_id=2, has_side_effects=True, vmem_limit_bytes=VMEM_MAX),
        cost_estimate=pl.CostEstimate(flops=12 * n_rows * D * F, bytes_accessed=8 * n_rows * F, transcendentals=0),
        name='bwd_pipe',
    )(dh, xs, w_in, w_out)


def head_tile(et, base, nall_ref, lse_ref, tgt_ref, block):
    D = et.shape[1]
    c2 = D ** -0.5 * math.log2(math.e)
    k = 0.5 * D ** -0.5
    acc = None
    for j in range(0, nall_ref.shape[0], block):
        nb = nall_ref[j:j + block, :]
        q = jnp.exp2(mm_t(et, nb) * c2 - (lse_ref[:, j:j + block] - math.log2(k)))
        hit = lax.broadcasted_iota(jnp.int32, q.shape, 0) == tgt_ref[:, j:j + block] - base
        part = mm(jnp.where(hit, q - k, q).astype(BF), nb)
        acc = part if acc is None else acc + part
    return acc


def shard_kernel(block, off_ref, e_ref, nall_ref, lse_ref, tgt_ref, o_ref):
    tv = e_ref.shape[0]
    base = (off_ref[0] + pl.program_id(0)) * tv
    o_ref[...] = head_tile(e_ref[...], base, nall_ref, lse_ref, tgt_ref, block)


def head_shard(tv, n_tile, block, off, emb, nall, lse, tgt):
    D = emb.shape[1]
    return pl.pallas_call(
        functools.partial(shard_kernel, block),
        out_shape=jax.ShapeDtypeStruct((n_tile * tv, D), F32),
        grid_spec=pltpu.PrefetchScalarGridSpec(
            num_scalar_prefetch=1, grid=(n_tile,),
            in_specs=[pl.BlockSpec((tv, D), lambda i, o: (o[0] + i, 0)), VMEM, VMEM, VMEM],
            out_specs=pl.BlockSpec((tv, D), lambda i, o: (i, 0))),
        compiler_params=pltpu.CompilerParams(vmem_limit_bytes=VMEM_MAX),
        cost_estimate=pl.CostEstimate(flops=4 * n_tile * tv * D * nall.shape[0], bytes_accessed=6 * n_tile * tv * D, transcendentals=n_tile * tv * nall.shape[0]),
        name='head_shard',
    )(off, emb, nall, lse, tgt)


def add_rows(o_ref, base, lo, hi, ids_ref, mats):
    tv = o_ref.shape[0]

    def body(b, carry):
        hit = lax.broadcasted_iota(jnp.int32, (tv, 128), 0) == ids_ref[pl.ds(b, 1), :] - base
        oh = jnp.where(hit, 1.0, 0.0).astype(BF)
        part = None
        for m in mats:
            p = mm(oh, m[rows(b, 128), :])
            part = p if part is None else part + p
        o_ref[...] += part
        return carry

    lax.fori_loop(lo, hi, body, 0)


def local_kernel(block, tile0, lim_ref, e_ref, nall_ref, lse_ref, tgt_ref, ids_ref, dx_ref, lids_ref, g0_ref, g1_ref, g2_ref, o_ref):
    tv = e_ref.shape[0]
    t = pl.program_id(0) + tile0
    base = t * tv
    o_ref[...] = head_tile(e_ref[...], base, nall_ref, lse_ref, tgt_ref, block)
    add_rows(o_ref, base, lim_ref[0, t], lim_ref[1, t], ids_ref, (dx_ref,))
    add_rows(o_ref, base, lim_ref[2, t], lim_ref[3, t], lids_ref, (g0_ref, g1_ref, g2_ref))


def local_part(tv, tile0, block, lim, emb, nall, lse, tgt, ids, dx, lids, g3):
    V, D = emb.shape
    n_tile = pl.cdiv(V, tv) - tile0
    return pl.pallas_call(
        functools.partial(local_kernel, block, tile0),
        out_shape=jax.ShapeDtypeStruct((V, D), F32),
        grid=(n_tile,),
        in_specs=[SMEM, pl.BlockSpec((tv, D), lambda i: (i + tile0, 0))] + [VMEM] * 9,
        out_specs=pl.BlockSpec((tv, D), lambda i: (i + tile0, 0)),
        compiler_params=pltpu.CompilerParams(vmem_limit_bytes=VMEM_MAX),
        cost_estimate=pl.CostEstimate(flops=4 * n_tile * tv * D * nall.shape[0], bytes_accessed=6 * n_tile * tv * D, transcendentals=n_tile * tv * nall.shape[0]),
        name='head_local',
    )(lim, emb, nall, lse, tgt, ids, dx, lids, *g3)


def sweep_kernel(lim_ref, full_ref, a_ref, ids_ref, dx_ref, lids_ref, g0_ref, g1_ref, g2_ref, o_ref):
    t = pl.program_id(0)
    base = t * o_ref.shape[0]
    o_ref[...] = a_ref[...]
    add_rows(o_ref, base, lim_ref[0, t], lim_ref[1, t], ids_ref, (dx_ref,))
    add_rows(o_ref, base, lim_ref[2, t], lim_ref[3, t], lids_ref, (g0_ref, g1_ref, g2_ref))


def sweep(tv, lim, full, gathered, ids, dx, lids, g3):
    n, D = gathered.shape
    return pl.pallas_call(
        sweep_kernel,
        out_shape=jax.ShapeDtypeStruct(full.shape, F32),
        grid=(n // tv,),
        in_specs=[SMEM, ANY, pl.BlockSpec((tv, D), lambda i: (i, 0))] + [VMEM] * 6,
        out_specs=pl.BlockSpec((tv, D), lambda i: (i, 0)),
        input_output_aliases={1: 0},
        compiler_params=pltpu.CompilerParams(vmem_limit_bytes=VMEM_MAX),
        cost_estimate=pl.CostEstimate(flops=n * D, bytes_accessed=8 * n * D, transcendentals=0),
        name='sweep',
    )(lim, full, gathered, ids, dx, lids, *g3)


def limits(sorted_ids, tv, n_tile):
    edge = jnp.arange(n_tile + 1, dtype=jnp.int32) * tv
    below = jnp.sum((sorted_ids[None, :] < edge[:, None]).astype(jnp.int32), axis=1)
    lo, hi = below[:-1], below[1:]
    return lo // 128, jnp.where(hi > lo, (hi + 127) // 128, lo // 128)


SHARED = 0.64
TILE_V = 512


def solution(mesh):
    S = mesh.shape[AXIS]

    def per_device(token_ids, label_ids, label2_ids, embed_table, w_up, w_down, mtp_up, mtp_down):
        V, D = embed_table.shape
        N = token_ids.size
        R = N // S
        me = lax.axis_index(AXIS)
        w_in, w_out = w_up[0], w_down[0]

        tok, lab, lab2 = lax.sort((token_ids.reshape(N), label_ids.reshape(N), label2_ids.reshape(N)), num_keys=1)
        lab_sorted, lab_perm = lax.sort((lab, lax.iota(jnp.int32, N)), num_keys=1)

        def own(v):
            return lax.dynamic_slice_in_dim(v, me * R, R)

        picked = embed_table[jnp.concatenate([own(tok), own(lab), own(lab2)])]
        x_own, e1, e2 = picked[:R], picked[R:2 * R], picked[2 * R:]
        xs, h_own = forward(S, R, 1024, x_own, w_in, w_out)
        tg = jnp.concatenate([own(lab), own(lab2)]).reshape(2 * R, 1)
        nall, lall, dh, dg = heads(S, 1024, 1024, h_own, e1, e2, tg, mtp_up, mtp_down, embed_table)
        nall = nall.reshape(2 * N, D)
        lse = lall[:, 0, :].reshape(1, 2 * N)
        loss = (0.5 * jnp.sum(lall[:, 1, 0]) / N).reshape(1)
        tgt = jnp.stack([lab.reshape(S, R), lab2.reshape(S, R)], axis=1).reshape(1, 2 * N)

        dg_all = lax.all_gather(dg, AXIS, axis=0, tiled=True)
        n_tile = pl.cdiv(V, TILE_V)
        shard_tiles = int(V * SHARED) // (S * TILE_V)
        n_shared = shard_tiles * S
        mine = head_shard(TILE_V, shard_tiles, 1024, (me * shard_tiles).reshape(1), embed_table, nall, lse, tgt)
        gathered = lax.all_gather(mine, AXIS, axis=0, tiled=True)

        dsv, dpre, hid, dx = backward(S, R, 1024, dh, xs, w_in, w_out)
        g_up = lax.dot_general(xs, dpre, (((0,), (0,)), ((), ())), preferred_element_type=F32)
        g_down = lax.dot_general(hid, dsv, (((0,), (0,)), ((), ())), preferred_element_type=F32)

        dg_rows = dg_all[lab_perm]
        g0 = dg_rows.astype(BF)
        r1 = dg_rows - lax.reduce_precision(dg_rows, 8, 7)
        g1 = r1.astype(BF)
        g2 = (r1 - lax.reduce_precision(r1, 8, 7)).astype(BF)
        lim = jnp.stack(limits(tok, TILE_V, n_tile) + limits(lab_sorted, TILE_V, n_tile))
        ids = tok.reshape(N // 128, 128)
        lids = lab_sorted.reshape(N // 128, 128)
        full = local_part(TILE_V, n_shared, 1024, lim, embed_table, nall, lse, tgt, ids, dx, lids, (g0, g1, g2))
        grad_emb = sweep(TILE_V, lim, full, gathered, ids, dx, lids, (g0, g1, g2))
        return loss, g_up[None], g_down[None], grad_emb

    in_specs = (P('dp', None), P('dp', None), P('dp', None), P(None, None), P('stage', None, None), P('stage', None, None), P(None, None), P(None, None))
    out_specs = (P('dp'), P(('dp', 'stage'), None, None), P(('dp', 'stage'), None, None), P('dp', None))
    return jax.shard_map(per_device, mesh=mesh, in_specs=in_specs, out_specs=out_specs, check_vma=False)
```

time: 3670 us -> 703 us (0.19)
  the two profiles are of different devices: /device:TPU:112 before, /device:TPU:117 now
where the time goes in v1:
time: 703 us; the launch traced here: 693 us
  Pallas kernels  607 us (86%)
  matrix products  27.1 us (4%)
  local copies, waits for them, and re-layouts  23.2 us (3%)
  other arithmetic  18.4 us (3%)
  between operations  16.4 us (2%)
    pallas_call x1, Pallas kernels, backward(): pl.pallas_call(functools.partial(bwd_kernel, S, C, tile), out_shape=(jax....  205 us
    pallas_call x1, Pallas kernels, local_part(): pl.pallas_call(functools.partial(local_kernel, block, tile0), out_shape=j...  142 us
    pallas_call x1, Pallas kernels, heads(): pl.pallas_call(functools.partial(heads_kernel, S, TV, tile), out_shape=(j...  97.3 us
    pallas_call x1, Pallas kernels, forward(): pl.pallas_call(functools.partial(fwd_kernel, S, C, tile), out_shape=(jax....  69.1 us
    pallas_call x1, Pallas kernels, sweep(): pl.pallas_call(sweep_kernel, out_shape=jax.ShapeDtypeStruct(full.shape, F...  65.2 us
    pallas_call x1, Pallas kernels, head_shard(): pl.pallas_call(functools.partial(shard_kernel, block), out_shape=jax.Shap...  28.2 us
    dot_general x1, matrix products, per_device(): lax.dot_general(xs, dpre, (((0,), (0,)), ((), ())), preferred_element_typ...  15.3 us
  transfers between devices with their start and end apart: 2, of which 0 were waited for; matrix products, arithmetic and copies ran while one was open for 8% of the time, Pallas kernels for 54%

profile of v1, /device:TPU:117, one launch (start us, length us, event | category | flops | bytes accessed | tf_op | source)
XLA Modules:
  0.0 692.6 jit_solution(13899734526385360506)
XLA Ops:
  7.2 0.1 all-gather.3.cloned.1.call-start
  7.3 0.7 copy.15
  8.0 0.7 copy.16
  8.7 0.7 copy.17
  9.4 5.1 sort.46
  14.5 0.0 copy-start
  14.5 0.1 dynamic_slice.13
  14.6 0.1 dynamic_slice.12
  14.7 0.1 dynamic_slice.11
  14.8 0.9 copy.14.tg_ref
  15.6 5.2 gather_fusion
  20.9 0.9 fusion.6
  21.8 69.1 %fwd_pipe.1 = (bf16[2048,512]{1,0:T(8,128)(2,1)}, bf16[256,512]{1,0:T(8,128)(2,1)}) custom-call(bf16[256,512]{1,0:T(8,128)(2,1)} %get-tuple-element.48.x_ref, bf16[512,4096]{1,0:T(8,128)(2,1)} %bitcast.54, bf16[4096,512]{1,0:T(8,128)(2,1)} %bitcast.56), custom_call_target="tpu_custom_call" | custom-call | flops 17179869184 | bytes 8388608 | tf_op jit(solution)/shard_map/fwd_pipe/pallas_call | solution.py:143
  90.9 97.3 %heads.1 = (bf16[8,512,512]{2,1,0:T(8,128)(2,1)}, f32[8,8,512]{2,1,0:T(8,128)}, bf16[256,512]{1,0:T(8,128)(2,1)}, f32[256,512]{1,0:T(8,128)}) custom-call(bf16[256,512]{1,0:T(8,128)(2,1)} %get-tuple-element.25.h_ref, bf16[256,512]{1,0:T(8,128)(2,1)} %get-tuple-element.47.e1_ref, bf16[256,512]{1,0:T(8,128)(2,1)} %get-tuple-element.46.e2_ref, ...), custom_call_target="tpu_custom_call" | custom-call | flops 50532974592 | bytes 65798144 | tf_op jit(solution)/shard_map/heads/pallas_call | solution.py:283
  188.2 0.1 all-gather.3.cloned.1.call-update
  188.3 0.1 all-gather.5.cloned.1.call-start
  188.4 0.6 reshape.170.tgt_ref
  189.0 1.5 slice.35
  190.5 28.2 %head_shard.1 = f32[2560,512]{1,0:T(8,128)} custom-call(s32[1]{0:T(128)} %bitcast.19.off_ref, bf16[32128,512]{1,0:T(8,128)(2,1)} %e_ref.3, bf16[4096,512]{1,0:T(8,128)(2,1)} %bitcast.58, f32[1,4096]{1,0:T(1,128)} %bitcast.42, s32[1,4096]{1,0:T(1,128)} %reshape.170.tgt_ref), custom_call_target="tpu_custom_call" | custom-call | flops 21474836480 | bytes 7864320 | tf_op jit(solution)/shard_map/head_shard/pallas_call | solution.py:469
  218.7 0.1 all-gather.5.cloned.1.call-update
  218.8 4.4 sort.47
  223.2 0.0 copy-start.1
  223.2 1.4 slice_reduce_fusion
  225.2 0.0 copy-done
  225.2 0.3 convert_reduce_fusion.1
  225.5 0.1 fusion.4
  225.6 0.5 pad_add_fusion.2.lim_ref
  226.2 205.0 %bwd_pipe.1 = (bf16[2048,512]{1,0:T(8,128)(2,1)}, bf16[2048,4096]{1,0:T(8,128)(2,1)}, bf16[2048,4096]{1,0:T(8,128)(2,1)}, bf16[2048,512]{1,0:T(8,128)(2,1)}) custom-call(bf16[256,512]{1,0:T(8,128)(2,1)} %get-tuple-element.28.dh_ref, bf16[2048,512]{1,0:T(8,128)(2,1)} %get-tuple-element.27.xs_ref, bf16[512,4096]{1,0:T(8,128)(2,1)} %bitcast.55, ...), custom_call_target="tpu_custom_call" | custom-call | flops 51539607552 | bytes 67108864 | tf_op jit(solution)/shard_map/bwd_pipe/pallas_call | solution.py:423
  431.2 0.0 copy-done.1
  431.2 0.0 copy-start.2
  431.2 0.0 copy-start.3
  431.2 15.3 %convolution_bitcast_fusion.1 = f32[1,512,4096]{2,1,0:T(8,128)} fusion(bf16[2048,512]{1,0:T(8,128)(2,1)} %get-tuple-element.27.xs_ref, bf16[2048,4096]{1,0:T(8,128)(2,1)} %get-tuple-element.29), kind=kOutput, calls=%fused_computation.3 | convolution fusion | flops 8589934592 | bytes 27262976 | tf_op jit(solution)/shard_map/dot_general | solution.py:590
  446.5 0.0 copy-done.2
  446.5 0.0 copy-done.3
  446.5 11.8 %convolution_bitcast_fusion = f32[1,4096,512]{2,1,0:T(8,128)} fusion(bf16[2048,4096]{1,0:T(8,128)(2,1)S(1)} %copy-done.2, bf16[2048,512]{1,0:T(8,128)(2,1)S(1)} %copy-done.3), kind=kOutput, calls=%fused_computation.2 | convolution fusion | flops 8589934592 | bytes 27262976 | tf_op jit(solution)/shard_map/dot_general | solution.py:591
  458.3 0.0 all-gather.3.cloned.1.call-done
  458.3 11.7 %gather_fusion.1 = f32[2048,512]{1,0:T(8,128)} fusion(f32[2048,512]{1,0:T(8,128)} %all-gather.3.cloned.1.call-done, s32[2048]{0:T(1024)S(1)} %fusion.2), kind=kCustom, calls=%fused_computation.1 | custom fusion | bytes 8396800 | tf_op jit(solution)/shard_map/gather | solution.py:593
  470.0 6.5 fusion
  476.5 142.4 %head_local.1.full_ref = f32[32128,512]{1,0:T(8,128)} custom-call(s32[4,63]{1,0:T(4,128)} %pad_add_fusion.2.lim_ref, bf16[32128,512]{1,0:T(8,128)(2,1)} %e_ref.3, bf16[4096,512]{1,0:T(8,128)(2,1)} %bitcast.59, f32[1,4096]{1,0:T(1,128)} %bitcast.43, s32[1,4096]{1,0:T(1,128)} %reshape.170.tgt_ref, s32[16,128]{1,0:T(8,128)} %bitcast.34, ...), custom_call_target="tpu_custom_call" | custom-call | flops 98784247808 | bytes 36175872 | tf_op jit(solution)/shard_map/head_local/pallas_call | solution.py:510
  619.0 0.0 all-gather.5.cloned.1.call-done.a_ref
  619.0 65.2 %sweep.1 = f32[32128,512]{1,0:T(8,128)} custom-call(s32[4,63]{1,0:T(4,128)} %pad_add_fusion.2.lim_ref, f32[32128,512]{1,0:T(8,128)} %head_local.1.full_ref, f32[20480,512]{1,0:T(8,128)} %all-gather.5.cloned.1.call-done.a_ref, s32[16,128]{1,0:T(8,128)} %bitcast.35, bf16[2048,512]{1,0:T(8,128)(2,1)} %get-tuple-element.34.dx_ref, ...), custom_call_target="tpu_custom_call", output_to_operand_aliasing={{}: (1, {})} | custom-call | flops 10485760 | bytes 83886080 | tf_op jit(solution)/shard_map/sweep/pallas_call | solution.py:532
  (8 shorter events, 0.1 us)
Async XLA Ops:
  7.2 451.1 %all-gather.3.cloned.1.call-start = ((), (), s32[]{:S(2)}) async-start(), calls=%async_computation | async-start | bytes 4718592 | tf_op jit(solution)/shard_map/all_gather | solution.py:582
  14.5 210.7 %copy-start = (s32[2048]{0:T(1024)}, s32[2048]{0:T(1024)S(1)}, u32[]{:S(2)}) copy-start(s32[2048]{0:T(1024)S(1)} %get-tuple-element.22) | copy-start | bytes 24580
  188.3 430.7 %all-gather.5.cloned.1.call-start = ((), (), s32[]{:S(2)}) async-start(), calls=%async_computation.1 | async-start | bytes 47185920 | tf_op jit(solution)/shard_map/all_gather | solution.py:587
  223.2 208.0 %copy-start.1 = (s32[2048]{0:T(1024)}, s32[2048]{0:T(1024)S(1)}, u32[]{:S(2)}) copy-start(s32[2048]{0:T(1024)S(1)} %get-tuple-element.32) | copy-start | bytes 24580
  431.2 15.3 %copy-start.2 = (bf16[2048,4096]{1,0:T(8,128)(2,1)S(1)}, bf16[2048,4096]{1,0:T(8,128)(2,1)}, u32[]{:S(2)}) copy-start(bf16[2048,4096]{1,0:T(8,128)(2,1)} %get-tuple-element.30) | copy-start | bytes 50331652
  431.2 15.3 %copy-start.3 = (bf16[2048,512]{1,0:T(8,128)(2,1)S(1)}, bf16[2048,512]{1,0:T(8,128)(2,1)}, u32[]{:S(2)}) copy-start(bf16[2048,512]{1,0:T(8,128)(2,1)} %get-tuple-element.31) | copy-start | bytes 6291460
Sparse Core Ops, SparseCore 0:
  188.4 28.4 all-gather.2
  218.9 211.8 all-gather.4

commit v2 on v1

v2 whole, which is shorter than its diff:
```python
import functools
import math

import jax
import jax.numpy as jnp
from jax import lax
from jax.experimental import pallas as pl
from jax.experimental.pallas import tpu as pltpu
from jax.sharding import PartitionSpec as P


EPS_NORM = 1e-6
BF = jnp.bfloat16
F32 = jnp.float32
AXIS = 'stage'
GELU_A = math.sqrt(2.0 / math.pi)
GELU_B = 0.044715
VMEM_MAX = 67000000
DEPTH = 4

VMEM = pl.BlockSpec(memory_space=pltpu.VMEM)
ANY = pl.BlockSpec(memory_space=pl.ANY)
SMEM = pl.BlockSpec(memory_space=pltpu.SMEM)
NN = (((1,), (0,)), ((), ()))
NT = (((1,), (1,)), ((), ()))


def cost(work, elems):
    return pl.CostEstimate(flops=8 * work, bytes_accessed=8 * elems, transcendentals=0)


def mm(a, b):
    return lax.dot_general(a, b, NN, preferred_element_type=F32)


def mm_t(a, b):
    return lax.dot_general(a, b, NT, preferred_element_type=F32)


def gelu(v):
    return 0.5 * v * (1.0 + jnp.tanh(GELU_A * (v + GELU_B * (v * v * v))))


def gelu_both(v):
    sq = v * v
    t = jnp.tanh(GELU_A * (v + GELU_B * (sq * v)))
    half = 0.5 * (1.0 + t)
    slope = half + (0.5 * v) * (1.0 - t * t) * (GELU_A * (1.0 + (3.0 * GELU_B) * sq))
    return v * half, slope


def dev(d):
    return {AXIS: d}


def greet_all(n_dev):
    me = lax.axis_index(AXIS)
    bar = pltpu.get_barrier_semaphore()
    for d in range(1, n_dev):
        pl.semaphore_signal(bar, inc=1, device_id=dev(lax.rem(me + d, n_dev)), device_id_type=pl.DeviceIdType.MESH)
    pl.semaphore_wait(bar, n_dev - 1)
    return me


def rcopy(src, dst, ssem, rsem, d):
    return pltpu.make_async_remote_copy(src_ref=src, dst_ref=dst, send_sem=ssem, recv_sem=rsem, device_id=dev(d), device_id_type=pl.DeviceIdType.MESH)


def rows(c, size):
    return pl.ds(pl.multiple_of(c * size, size), size)


def mlp_rows(x, wi_ref, wo_ref, tile):
    acc = None
    for f in range(0, wi_ref.shape[1], tile):
        hid = gelu(mm(x, wi_ref[:, f:f + tile])).astype(BF)
        part = mm(hid, wo_ref[f:f + tile, :])
        acc = part if acc is None else acc + part
    return (x.astype(F32) + acc).astype(BF)


def fwd_kernel(S, C, tile, x_ref, wi_ref, wo_ref, xs_ref, h_ref, wit_ref, wot_ref, ob, own_sem, send_sem, recv_sem, h_sem):
    n_rows = xs_ref.shape[0]
    own = x_ref.shape[0]
    n_chunk, per = n_rows // C, own // C
    me = greet_all(S)
    nxt = lax.rem(me + 1, S)

    def flip(f, carry):
        wit_ref[rows(f, 512), :] = jnp.transpose(wi_ref[:, rows(f, 512)])
        wot_ref[:, rows(f, 512)] = jnp.transpose(wo_ref[rows(f, 512), :])
        return carry

    early = me >= S // 2

    @pl.when(me > 0)
    def _():
        for j in range(per):
            rcopy(x_ref.at[rows(j, C)], xs_ref.at[rows(me * per + j, C)], own_sem.at[j], recv_sem.at[me * per + j], 0).start()

    @pl.when(me == 0)
    def _():
        xs_ref[0:own, :] = x_ref[...]

    lax.fori_loop(0, jnp.where(early, wi_ref.shape[1] // 512, 0), flip, 0)

    def step(c, carry):
        @pl.when((me > 0) | (c >= per))
        def _():
            rcopy(xs_ref.at[rows(c, C)], xs_ref.at[rows(c, C)], send_sem.at[c], recv_sem.at[c], nxt).wait_recv()

        ob[rows(c, C), :] = mlp_rows(xs_ref[rows(c, C), :], wi_ref, wo_ref, tile)
        owner = c // per
        j = lax.rem(c, per)

        @pl.when(me < S - 1)
        def _():
            rcopy(ob.at[rows(c, C)], xs_ref.at[rows(c, C)], send_sem.at[c], recv_sem.at[c], nxt).start()

        @pl.when((me == S - 1) & (owner < S - 1))
        def _():
            rcopy(ob.at[rows(c, C)], h_ref.at[rows(j, C)], send_sem.at[c], h_sem.at[j], owner).start()

        @pl.when((me == S - 1) & (owner == S - 1))
        def _():
            h_ref[rows(j, C), :] = ob[rows(c, C), :]

        return carry

    lax.fori_loop(0, n_chunk, step, 0)

    @pl.when(me > 0)
    def _():
        for j in range(per):
            rcopy(x_ref.at[rows(j, C)], xs_ref.at[rows(me * per + j, C)], own_sem.at[j], recv_sem.at[me * per + j], 0).wait_send()

    def drain(c, carry):
        @pl.when((me < S - 1) | (c < (S - 1) * per))
        def _():
            rcopy(ob.at[rows(c, C)], xs_ref.at[rows(c, C)], send_sem.at[c], recv_sem.at[c], nxt).wait_send()

        return carry

    lax.fori_loop(0, jnp.where(early, 0, wi_ref.shape[1] // 512), flip, 0)
    lax.fori_loop(0, n_chunk, drain, 0)

    @pl.when(me < S - 1)
    def _():
        for j in range(per):
            rcopy(ob.at[rows(j, C)], h_ref.at[rows(j, C)], send_sem.at[j], h_sem.at[j], nxt).wait_recv()


def forward(S, C, tile, x_own, w_in, w_out):
    own, width = x_own.shape
    n_rows = own * S
    n_chunk, per = n_rows // C, own // C
    return pl.pallas_call(
        functools.partial(fwd_kernel, S, C, tile),
        out_shape=(jax.ShapeDtypeStruct((n_rows, width), BF), jax.ShapeDtypeStruct((own, width), BF),
                   jax.ShapeDtypeStruct(w_out.shape, BF), jax.ShapeDtypeStruct(w_in.shape, BF)),
        in_specs=[VMEM] * 3,
        out_specs=(VMEM,) * 4,
        scratch_shapes=[
            pltpu.VMEM((n_rows, width), BF),
            pltpu.SemaphoreType.DMA((per,)),
            pltpu.SemaphoreType.DMA((n_chunk,)),
            pltpu.SemaphoreType.DMA((n_chunk,)),
            pltpu.SemaphoreType.DMA((per,)),
        ],
        compiler_params=pltpu.CompilerParams(collective_id=0, has_side_effects=True, vmem_limit_bytes=VMEM_MAX),
        cost_estimate=cost(n_rows * w_in.size, w_in.size),
        name='fwd_pipe',
    )(x_own, w_in, w_out)


def stream(emb_ref, ebuf, esem, TV):
    def fetch(i):
        slot = lax.rem(i, ebuf.shape[0])
        return pltpu.make_async_copy(emb_ref.at[rows(i, TV)], ebuf.at[slot], esem.at[slot])

    return fetch


def staged(n_full, first, stage, last):
    first()

    def pair(j, carry):
        carry = stage(2 * j + 1, 1, 0, carry)
        return stage(2 * j + 2, 0, 1, carry)

    return lambda carry: tail(n_full, stage, last, lax.fori_loop(0, (n_full - 1) // 2, pair, carry))


def tail(n_full, stage, last, carry):
    if (n_full - 1) % 2:
        carry = stage(n_full - 1, 1, 0, carry)
    return last((n_full - 1) % 2, carry)


def lse_kernel(S, TV, tile, h_ref, e1_ref, e2_ref, wi_ref, wo_ref, emb_ref,
               nall_ref, lall_ref, st_ref, lcol_ref,
               ebuf, erem, la, lb, lrow, esem, rsem, nsend, nrecv, lsend, lrecv):
    R, D = h_ref.shape
    V = emb_ref.shape[0]
    n_full = V // TV
    rem = V - n_full * TV
    scale = D ** -0.5
    c2 = scale * math.log2(math.e)
    me = greet_all(S)
    fetch = stream(emb_ref, ebuf, esem, TV)
    for i in range(DEPTH):
        fetch(i).start()
    rem_copy = pltpu.make_async_copy(emb_ref.at[pl.ds(n_full * TV, rem)], erem, rsem)
    rem_copy.start()

    hf = h_ref[...].astype(F32)
    st_ref[0:R, :] = h_ref[...]
    g_in = (hf + e1_ref[...].astype(F32)).astype(BF)
    acc_ref = la.at[pl.ds(0, R)]
    acc_ref[...] = jnp.zeros((R, D), F32)

    def mtp(f, carry):
        acc_ref[...] += mm(gelu(mm(g_in, wi_ref[:, rows(f, tile)])).astype(BF), wo_ref[rows(f, tile), :])
        return carry

    lax.fori_loop(0, wi_ref.shape[1] // tile, mtp, 0)
    g_out = (g_in.astype(F32) + acc_ref[...]).astype(BF)
    st_ref[R:, :] = g_out
    for j, v in enumerate((hf, g_out.astype(F32))):
        inv = lax.rsqrt(jnp.mean(v * v, axis=-1, keepdims=True) + EPS_NORM)
        nall_ref[me, j * R:(j + 1) * R, :] = (v * inv).astype(BF)

    sib = me + 1 - 2 * lax.rem(me, 2)

    def block(b, ssem, d):
        return rcopy(nall_ref.at[b], nall_ref.at[b], ssem, nrecv.at[b], d)

    def peer(d):
        return lax.rem(me + 2 * d, S)

    def lcopy(d):
        return rcopy(lall_ref.at[me], lall_ref.at[me], lsend.at[d], lrecv.at[d], lax.rem(me + d, S))

    for d in range(1, S // 2):
        block(me, nsend.at[d], peer(d)).start()
    block(me, nsend.at[0], sib).start()

    bufs = (la, lb)

    def fold(lt, mx, sm):
        grp = lt.reshape(lt.shape[0] // 8, 8, 2 * R)
        new = jnp.maximum(mx, jnp.max(grp, axis=0))
        sm = sm * jnp.exp2((mx - new) * c2) + jnp.sum(jnp.exp2((grp - new[None]) * c2), axis=0)
        return new, sm

    def first():
        fetch(0).wait()
        la[...] = mm_t(ebuf[0], nall_ref[me])

    def stage(i, w, r, carry):
        fetch(i).wait()

        @pl.when(i + DEPTH - 1 < n_full)
        def _():
            fetch(i + DEPTH - 1).start()

        bufs[w][...] = mm_t(ebuf[lax.rem(i, ebuf.shape[0])], nall_ref[me])
        return fold(bufs[r][...], *carry)

    def last(r, carry):
        return fold(bufs[r][...], *carry)

    mx, sm = staged(n_full, first, stage, last)((jnp.full((8, 2 * R), -jnp.inf, F32), jnp.zeros((8, 2 * R), F32)))
    for d in range(1, S // 2):
        block(peer(d), nsend.at[S // 2 + d], sib).wait_recv()
        block(peer(d), nsend.at[S // 2 + d], sib).start()
    rem_copy.wait()
    mx, sm = fold(mm_t(erem[...], nall_ref[me]), mx, sm)
    top = jnp.max(mx, axis=0, keepdims=True)
    tot = jnp.sum(sm * jnp.exp2((mx - top) * c2), axis=0, keepdims=True)
    lse2 = top * c2 + jnp.log(tot) * math.log2(math.e)
    lrow[...] = jnp.broadcast_to(lse2, (128, 2 * R))
    lcol_ref[...] = jnp.transpose(lrow[...])
    nrm = nall_ref[me].astype(F32)
    pick = jnp.concatenate([
        jnp.sum(nrm[:R] * e1_ref[...].astype(F32), axis=-1, keepdims=True),
        jnp.sum(nrm[R:] * e2_ref[...].astype(F32), axis=-1, keepdims=True)], axis=0) * scale
    nll = jnp.sum(lcol_ref[:, 0:1] * math.log(2.0) - pick, axis=0, keepdims=True)
    lall_ref[me] = jnp.where(lax.broadcasted_iota(jnp.int32, (8, 2 * R), 0) == 0, jnp.broadcast_to(lse2, (8, 2 * R)), jnp.broadcast_to(nll, (8, 2 * R)))
    for d in range(1, S):
        lcopy(d).start()
    for d in range(1, S // 2):
        block(me, nsend.at[d], peer(d)).wait_send()
        block(peer(d), nsend.at[S // 2 + d], sib).wait_send()
        block(lax.rem(sib + 2 * d, S), nsend.at[d], sib).wait_recv()
    block(me, nsend.at[0], sib).wait_send()
    block(sib, nsend.at[0], sib).wait_recv()
    for d in range(1, S):
        lcopy(d).wait_send()
        src = lax.rem(me + S - d, S)
        rcopy(lall_ref.at[me], lall_ref.at[src], lsend.at[d], lrecv.at[d], lax.rem(me + d, S)).wait_recv()


def lse_phase(S, TV, tile, h_own, e1, e2, mtp_up, mtp_down, emb):
    R, D = h_own.shape
    V = emb.shape[0]
    return pl.pallas_call(
        functools.partial(lse_kernel, S, TV, tile),
        out_shape=(jax.ShapeDtypeStruct((S, 2 * R, D), BF), jax.ShapeDtypeStruct((S, 8, 2 * R), F32),
                   jax.ShapeDtypeStruct((2 * R, D), BF), jax.ShapeDtypeStruct((2 * R, 128), F32)),
        in_specs=[VMEM] * 5 + [ANY],
        out_specs=(VMEM,) * 4,
        scratch_shapes=[
            pltpu.VMEM((DEPTH, TV, D), BF),
            pltpu.VMEM((V % TV, D), BF),
            pltpu.VMEM((TV, 2 * R), F32),
            pltpu.VMEM((TV, 2 * R), F32),
            pltpu.VMEM((128, 2 * R), F32),
            pltpu.SemaphoreType.DMA((DEPTH,)),
            pltpu.SemaphoreType.DMA,
            pltpu.SemaphoreType.DMA((S,)),
            pltpu.SemaphoreType.DMA((S,)),
            pltpu.SemaphoreType.DMA((S,)),
            pltpu.SemaphoreType.DMA((S,)),
        ],
        compiler_params=pltpu.CompilerParams(collective_id=1, has_side_effects=True, vmem_limit_bytes=VMEM_MAX),
        cost_estimate=cost(R * D * V, V * D),
        name='heads_lse',
    )(h_own, e1, e2, mtp_up, mtp_down, emb)


def grad_kernel(TV, tile, st_ref, e1_ref, tg_ref, lcol_ref, wi_ref, wo_ref, emb_ref, after_ref,
                dh_ref, dg_ref, ebuf, erem, la, lb, nb, dn_buf, esem, rsem):
    R, D = e1_ref.shape
    V = emb_ref.shape[0]
    n_full = V // TV
    rem = V - n_full * TV
    scale = D ** -0.5
    c2 = scale * math.log2(math.e)
    k = 0.5 * scale
    fetch = stream(emb_ref, ebuf, esem, TV)
    for i in range(DEPTH):
        fetch(i).start()
    rem_copy = pltpu.make_async_copy(emb_ref.at[pl.ds(n_full * TV, rem)], erem, rsem)
    rem_copy.start()
    stf = st_ref[...].astype(F32)
    inv = lax.rsqrt(jnp.mean(stf * stf, axis=-1, keepdims=True) + EPS_NORM)
    nb[...] = (stf * inv).astype(BF)
    shift = lcol_ref[:, 0:1] - math.log2(k)
    dn_buf[...] = jnp.zeros_like(dn_buf)
    bufs = (la, lb)

    def back(logit, et, base):
        n = logit.shape[1]
        q = jnp.exp2(logit * c2 - shift)
        hit = lax.broadcasted_iota(jnp.int32, (2 * R, n), 1) == tg_ref[...] - base
        dl = jnp.where(hit, q - k, q).astype(BF)
        dn_buf[...] += mm(dl, et)

    def first():
        fetch(0).wait()
        la[...] = mm_t(nb[...], ebuf[0])

    def stage(i, w, r, carry):
        fetch(i).wait()

        @pl.when(i + DEPTH - 1 < n_full)
        def _():
            fetch(i + DEPTH - 1).start()

        bufs[w][...] = mm_t(nb[...], ebuf[lax.rem(i, DEPTH + 1)])
        back(bufs[r][...], ebuf[lax.rem(i + DEPTH, DEPTH + 1)], (i - 1) * TV)
        return carry

    def last(r, carry):
        back(bufs[r][...], ebuf[(n_full - 1) % (DEPTH + 1)], (n_full - 1) * TV)
        return carry

    staged(n_full, first, stage, last)(0)
    rem_copy.wait()
    back(mm_t(nb[...], erem[...]), erem[...], n_full * TV)

    stf = st_ref[...].astype(F32)
    inv = lax.rsqrt(jnp.mean(stf * stf, axis=-1, keepdims=True) + EPS_NORM)
    nf = stf * inv
    dn = dn_buf[...]
    ds = inv * (dn - nf * jnp.mean(dn * nf, axis=-1, keepdims=True))
    dout = ds[R:].astype(BF)
    dn_buf[...] = ds
    g_in = (stf[:R] + e1_ref[...].astype(F32)).astype(BF)
    dg_ref[...] = dout.astype(F32)

    def mtp(f, carry):
        w1 = wi_ref[:, rows(f, tile)]
        _, slope = gelu_both(mm(g_in, w1))
        dpre = (mm_t(dout, wo_ref[rows(f, tile), :]) * slope).astype(BF)
        dg_ref[...] += mm_t(dpre, w1)
        return carry

    lax.fori_loop(0, wi_ref.shape[1] // tile, mtp, 0)
    dh_ref[...] = (dn_buf[0:R, :] + dg_ref[...]).astype(BF)


def grad_phase(TV, tile, st, e1, tg, lcol, mtp_up, mtp_down, emb, after):
    R, D = e1.shape
    V = emb.shape[0]
    return pl.pallas_call(
        functools.partial(grad_kernel, TV, tile),
        out_shape=(jax.ShapeDtypeStruct((R, D), BF), jax.ShapeDtypeStruct((R, D), F32)),
        in_specs=[VMEM] * 6 + [ANY] * 2,
        out_specs=(VMEM,) * 2,
        scratch_shapes=[
            pltpu.VMEM((DEPTH + 1, TV, D), BF),
            pltpu.VMEM((V % TV, D), BF),
            pltpu.VMEM((2 * R, TV), F32),
            pltpu.VMEM((2 * R, TV), F32),
            pltpu.VMEM((2 * R, D), BF),
            pltpu.VMEM((2 * R, D), F32),
            pltpu.SemaphoreType.DMA((DEPTH + 1,)),
            pltpu.SemaphoreType.DMA,
        ],
        compiler_params=pltpu.CompilerParams(vmem_limit_bytes=VMEM_MAX),
        cost_estimate=cost(R * D * V, V * D),
        name='heads_grad',
    )(st, e1, tg, lcol, mtp_up, mtp_down, emb, after)


def bwd_kernel(S, C, tile, row0, pre, dh_ref, xs_ref, wi_ref, wit_ref, wot_ref, nall_ref, lse_ref, tgt_ref, emb_ref, after_ref,
               ds_ref, dpre_ref, hid_ref, dx_ref, q_ref,
               ob, pbuf, hbuf, ebuf, acc_buf, esem, qsem, own_sem, send_sem, recv_sem, psem, hsem, bsend, brecv):
    n_rows = xs_ref.shape[0]
    own = dh_ref.shape[0]
    F = wi_ref.shape[1]
    n_chunk, per = n_rows // C, own // C
    me = greet_all(S)
    last = S - 1
    prv = lax.rem(me + S - 1, S)
    half = S // 2

    tv, _ = ebuf.shape[1:]
    nb, _, tb = lse_ref.shape
    n_q = q_ref.shape[0] // tv
    short = emb_ref.shape[0] - row0 - (n_q - 1) * tv
    n_unit = n_q * nb

    def fetch(t, go):
        slot = lax.rem(t, 2)

        @pl.when(t < n_q - 1)
        def _():
            cp = pltpu.make_async_copy(emb_ref.at[pl.ds(pl.multiple_of(row0 + t * tv, tv), tv)], ebuf.at[slot], esem.at[slot])
            cp.start() if go else cp.wait()

        @pl.when(t == n_q - 1)
        def _():
            cp = pltpu.make_async_copy(emb_ref.at[pl.ds(row0 + (n_q - 1) * tv, short)], ebuf.at[slot, pl.ds(0, short)], esem.at[slot])
            cp.start() if go else cp.wait()

    def q_copy(t):
        slot = lax.rem(t, 2)
        return pltpu.make_async_copy(acc_buf.at[slot], q_ref.at[rows(t, tv)], qsem.at[slot])

    def unit(u, carry):
        t = u // nb
        j = lax.rem(u, nb)
        slot = lax.rem(t, 2)

        @pl.when(j == 0)
        def _():
            fetch(t, False)
            fetch(t + 1, True)

            @pl.when(t >= 2)
            def _():
                q_copy(t - 2).wait()

        part = head_block(ebuf[slot], row0 + t * tv, nall_ref[rows(j, tb), :], lse_ref[j], tgt_ref[j])

        @pl.when(j == 0)
        def _():
            acc_buf[slot] = part

        @pl.when(j > 0)
        def _():
            acc_buf[slot] += part

        @pl.when(j == nb - 1)
        def _():
            q_copy(t).start()

        return carry

    def units(lo, hi):
        lax.fori_loop(jnp.minimum(lo, n_unit), jnp.minimum(hi, n_unit), unit, 0)

    fetch(0, True)

    @pl.when(me < last)
    def _():
        for j in range(per):
            rcopy(dh_ref.at[rows(j, C)], ds_ref.at[rows(me * per + j, C)], own_sem.at[j], recv_sem.at[me * per + j], last).start()

    @pl.when(me == last)
    def _():
        ds_ref[last * own:, :] = dh_ref[...]

    def spread(c, stop):
        def to(i, d):
            cp = rcopy(dx_ref.at[rows(c, C)], dx_ref.at[rows(c, C)], bsend.at[i, c], brecv.at[c], d)
            cp.wait_send() if stop else cp.start()

        @pl.when(lax.rem(me, 2) == 0)
        def _():
            to(0, me + 1)

        @pl.when((lax.rem(me, 2) == 0) & (me < half))
        def _():
            to(1, me + 2)

        @pl.when((me == 0) | ((lax.rem(me, 2) == 0) & (me > half + 2)))
        def _():
            to(2, lax.rem(me + S - 2, S))

    def out_copies(c):
        slot = lax.rem(c, 2)
        return (pltpu.make_async_copy(pbuf.at[slot], dpre_ref.at[rows(c, C)], psem.at[slot]),
                pltpu.make_async_copy(hbuf.at[slot], hid_ref.at[rows(c, C)], hsem.at[slot]))

    ahead = (last - me) * pre
    units(0, ahead)

    def step(c, carry):
        slot = lax.rem(c, 2)

        @pl.when(c >= 2)
        def _():
            for cp in out_copies(c - 2):
                cp.wait()

        @pl.when((me < last) | (c < last * per))
        def _():
            rcopy(ds_ref.at[rows(c, C)], ds_ref.at[rows(c, C)], send_sem.at[c], recv_sem.at[c], prv).wait_recv()

        x = xs_ref[rows(c, C), :]
        dout = ds_ref[rows(c, C), :]
        acc = dout.astype(F32)
        for f in range(0, F, tile):
            w1 = wi_ref[:, f:f + tile]
            hid, slope = gelu_both(mm(x, w1))
            dpre = (mm(dout, wot_ref[:, f:f + tile]) * slope).astype(BF)
            hbuf[slot, :, f:f + tile] = hid.astype(BF)
            pbuf[slot, :, f:f + tile] = dpre
            acc += mm(dpre, wit_ref[f:f + tile, :])
        res = acc.astype(BF)

        @pl.when(me > 0)
        def _():
            ob[rows(c, C), :] = res
            rcopy(ob.at[rows(c, C)], ds_ref.at[rows(c, C)], send_sem.at[c], recv_sem.at[c], prv).start()

        @pl.when(me == 0)
        def _():
            dx_ref[rows(c, C), :] = res
            spread(c, False)

        for cp in out_copies(c):
            cp.start()
        units(ahead + c, ahead + c + 1)
        return carry

    lax.fori_loop(0, n_chunk, step, 0)

    for c in (n_chunk - 2, n_chunk - 1):
        for cp in out_copies(c):
            cp.wait()

    @pl.when(me < last)
    def _():
        for j in range(per):
            rcopy(dh_ref.at[rows(j, C)], ds_ref.at[rows(me * per + j, C)], own_sem.at[j], recv_sem.at[me * per + j], last).wait_send()

    done = jnp.minimum(ahead + n_chunk, n_unit)
    left = (n_unit - done + n_chunk - 1) // n_chunk

    def drain(c, carry):
        @pl.when(me > 0)
        def _():
            rcopy(ob.at[rows(c, C)], ds_ref.at[rows(c, C)], send_sem.at[c], recv_sem.at[c], prv).wait_send()
            rcopy(dx_ref.at[rows(c, C)], dx_ref.at[rows(c, C)], bsend.at[0, c], brecv.at[c], prv).wait_recv()
            spread(c, False)

        units(done + c * left, done + (c + 1) * left)
        return carry

    lax.fori_loop(0, n_chunk, drain, 0)
    for t in range(max(n_q - 2, 0), n_q):
        q_copy(t).wait()

    def settle(c, carry):
        spread(c, True)
        return carry

    lax.fori_loop(0, n_chunk, settle, 0)
    dx_ref[n_rows:, :] = jnp.zeros((WIN, dx_ref.shape[1]), BF)


def backward(S, C, tile, row0, tv, pre, dh, xs, w_in, w_in_t, w_out_t, nall, lse, tgt, emb, after):
    own, D = dh.shape
    n_rows = xs.shape[0]
    F = w_in.shape[1]
    n_chunk, per = n_rows // C, own // C
    n_q = pl.cdiv(emb.shape[0] - row0, tv)
    return pl.pallas_call(
        functools.partial(bwd_kernel, S, C, tile, row0, pre),
        out_shape=(jax.ShapeDtypeStruct((n_rows, D), BF), jax.ShapeDtypeStruct((n_rows, F), BF),
                   jax.ShapeDtypeStruct((n_rows, F), BF), jax.ShapeDtypeStruct((n_rows + WIN, D), BF),
                   jax.ShapeDtypeStruct((n_q * tv, D), F32)),
        in_specs=[VMEM] * 8 + [ANY] * 2,
        out_specs=(VMEM, ANY, ANY, VMEM, ANY),
        scratch_shapes=[
            pltpu.VMEM((n_rows, D), BF),
            pltpu.VMEM((2, C, F), BF),
            pltpu.VMEM((2, C, F), BF),
            pltpu.VMEM((2, tv, D), BF),
            pltpu.VMEM((2, tv, D), F32),
            pltpu.SemaphoreType.DMA((2,)),
            pltpu.SemaphoreType.DMA((2,)),
            pltpu.SemaphoreType.DMA((per,)),
            pltpu.SemaphoreType.DMA((n_chunk,)),
            pltpu.SemaphoreType.DMA((n_chunk,)),
            pltpu.SemaphoreType.DMA((2,)),
            pltpu.SemaphoreType.DMA((2,)),
            pltpu.SemaphoreType.DMA((3, n_chunk)),
            pltpu.SemaphoreType.DMA((n_chunk,)),
        ],
        compiler_params=pltpu.CompilerParams(collective_id=2, has_side_effects=True, vmem_limit_bytes=VMEM_MAX),
        cost_estimate=cost(n_rows * w_in.size, n_rows * F),
        name='bwd_pipe',
    )(dh, xs, w_in, w_in_t, w_out_t, nall, lse, tgt, emb, after)


def head_block(et, base, rows_j, lse_j, tgt_j):
    D = et.shape[1]
    k = 0.5 * D ** -0.5
    q = jnp.exp2(mm_t(et, rows_j) * (D ** -0.5 * math.log2(math.e)) - (lse_j - math.log2(k)))
    hit = lax.broadcasted_iota(jnp.int32, q.shape, 0) == tgt_j - base
    return mm(jnp.where(hit, q - k, q).astype(BF), rows_j)


def shard_kernel(off_ref, e_ref, nall_ref, lse_ref, tgt_ref, after_ref, o_ref):
    tv = e_ref.shape[0]
    nb, _, tb = lse_ref.shape
    base = (off_ref[0] + pl.program_id(0)) * tv
    o_ref[...] = head_block(e_ref[...], base, nall_ref[0:tb, :], lse_ref[0], tgt_ref[0])

    def body(j, carry):
        o_ref[...] += head_block(e_ref[...], base, nall_ref[rows(j, tb), :], lse_ref[j], tgt_ref[j])
        return carry

    lax.fori_loop(1, nb, body, 0)


def head_shard(tv, n_tile, off, emb, nall, lse, tgt, after):
    D = emb.shape[1]
    return pl.pallas_call(
        shard_kernel,
        out_shape=jax.ShapeDtypeStruct((n_tile * tv, D), F32),
        grid_spec=pltpu.PrefetchScalarGridSpec(
            num_scalar_prefetch=1, grid=(n_tile,),
            in_specs=[pl.BlockSpec((tv, D), lambda i, o: (o[0] + i, 0)), VMEM, VMEM, VMEM, ANY],
            out_specs=pl.BlockSpec((tv, D), lambda i, o: (i, 0))),
        compiler_params=pltpu.CompilerParams(vmem_limit_bytes=VMEM_MAX),
        cost_estimate=cost(n_tile * tv * nall.size, n_tile * tv * D),
        name='head_shard',
    )(off, emb, nall, lse, tgt, after)


def split3(v):
    hi = v.astype(BF)
    rest = v - hi.astype(F32)
    mid = rest.astype(BF)
    return [hi, mid, (rest - mid.astype(F32)).astype(BF)]


def place(t, parts):
    at, base = t, 0
    for first, n in parts:
        at = jnp.where(t >= base, first + t - base, at)
        base += n
    return at


def sweep_kernel(tv, parts, lim_ref, tokw_ref, dx_ref, labw_ref, dg_ref, *refs):
    a_refs, o_ref = refs[:len(parts)], refs[-1]
    t = pl.program_id(0)
    tile0 = place(t, parts) * SUB
    top = tokw_ref.shape[0] - 1

    def part(s, i):
        tile = jnp.minimum(tile0 + s, lim_ref.shape[1] - 1)
        wt = jnp.minimum(lim_ref[0, tile] + i * (WIN // STEP), top)
        wl = jnp.minimum(lim_ref[1, tile] + i * (WIN // STEP), top)
        ids = jnp.maximum(tokw_ref[pl.ds(wt, 1), :], labw_ref[pl.ds(wl, 1), :]) - (tile0 + s) * tv
        hit = lax.broadcasted_iota(jnp.int32, (tv, 4 * WIN), 0) == ids
        near = pl.ds(pl.multiple_of(wt * STEP, STEP), WIN)
        far = pl.ds(pl.multiple_of(wl * STEP, STEP), WIN)
        return mm(jnp.where(hit, 1.0, 0.0).astype(BF), jnp.concatenate([dx_ref[near, :]] + split3(dg_ref[far, :]), axis=0))

    base = 0
    for (first, n), a_ref in zip(parts, a_refs):
        @pl.when((t >= base) & (t < base + n))
        def _():
            for s in range(SUB):
                o_ref[s * tv:(s + 1) * tv, :] = a_ref[s * tv:(s + 1) * tv, :] + part(s, 0)

        base += n

    for s in range(SUB):
        def more(i, carry):
            o_ref[s * tv:(s + 1) * tv, :] += part(s, i)
            return carry

        lax.fori_loop(1, lim_ref[2, jnp.minimum(tile0 + s, lim_ref.shape[1] - 1)], more, 0)


def sweep(tv, parts, arrays, lim, tokw, dx, labw, dg, out_rows, full):
    D = dx.shape[1]
    size = SUB * tv
    keep = [] if full is None else [full]
    specs, base = [], 0
    for first, n in parts:
        specs.append(pl.BlockSpec((size, D), lambda t, base=base, n=n: (jnp.clip(t - base, 0, n - 1), 0)))
        base += n
    return pl.pallas_call(
        functools.partial(sweep_kernel, tv, parts),
        out_shape=jax.ShapeDtypeStruct((out_rows, D), F32),
        grid=(base,),
        in_specs=[SMEM] + [VMEM] * 4 + specs + [ANY] * len(keep),
        out_specs=pl.BlockSpec((size, D), lambda t: (place(t, parts), 0)),
        input_output_aliases={5 + len(parts): 0} if keep else {},
        compiler_params=pltpu.CompilerParams(vmem_limit_bytes=VMEM_MAX),
        cost_estimate=cost(base * size * D, base * size * D),
        name='sweep',
    )(lim, tokw, dx, labw, dg, *arrays, *keep)


def windows(sorted_ids, slots):
    pad = jnp.pad(sorted_ids, (0, WIN), constant_values=-1).reshape(-1, STEP)
    n = sorted_ids.size // STEP
    win = jnp.concatenate([pad[i:i + n] for i in range(WIN // STEP)], axis=1)
    none = jnp.full_like(win, -1)
    return jnp.pad(jnp.concatenate([win if s else none for s in slots], axis=1), ((0, 1), (0, 0)), constant_values=-1)


def limits(tok, lab, tv, n_tile):
    edge = jnp.arange(n_tile + 1, dtype=jnp.int32) * tv

    def span(ids):
        below = jnp.sum((ids[None, :] < edge[:, None]).astype(jnp.int32), axis=1)
        w = below[:-1] // STEP
        return w, (below[1:] - w * STEP + WIN - 1) // WIN

    wt, nt = span(tok)
    wl, nl = span(lab)
    return jnp.stack([wt, wl, jnp.maximum(nt, nl)])


TILE_V = 512
TOKENS = 1024
WIN = 64
STEP = 16
AHEAD = 4
SUB = 2
PIECES = (2, 3, 1)
FWD_ROWS = 128
BWD_ROWS = 128


def solution(mesh):
    S = mesh.shape[AXIS]

    def per_device(token_ids, label_ids, label2_ids, embed_table, w_up, w_down, mtp_up, mtp_down):
        V, D = embed_table.shape
        N = token_ids.size
        R = N // S
        me = lax.axis_index(AXIS)
        w_in, w_out = w_up[0], w_down[0]

        tok, lab, lab2 = lax.sort((token_ids.reshape(N), label_ids.reshape(N), label2_ids.reshape(N)), num_keys=1)

        def own(v):
            return lax.dynamic_slice_in_dim(v, me * R, R)

        picked = embed_table[jnp.concatenate([own(tok), own(lab), own(lab2)])]
        x_own, e1, e2 = picked[:R], picked[R:2 * R], picked[2 * R:]
        xs, h_own, w_in_t, w_out_t = forward(S, FWD_ROWS, 1024, x_own, w_in, w_out)
        tg = jnp.concatenate([own(lab), own(lab2)]).reshape(2 * R, 1)
        nall, lall, st, lcol = lse_phase(S, 1024, 1024, h_own, e1, e2, mtp_up, mtp_down, embed_table)
        nall = nall.reshape(2 * N, D)
        lse = lall[:, 0, :].reshape(2 * N // TOKENS, 1, TOKENS)
        tgt = jnp.stack([lab.reshape(S, R), lab2.reshape(S, R)], axis=1).reshape(2 * N // TOKENS, 1, TOKENS)

        starts = [S * sum(PIECES[:i]) for i in range(len(PIECES) + 1)]

        def piece(i, after):
            off = (starts[i] + me * PIECES[i]).reshape(1)
            return head_shard(TILE_V, PIECES[i], off, embed_table, nall, lse, tgt, after)

        def share(v):
            return lax.all_gather(v, AXIS, axis=0, tiled=True)

        mine = [piece(0, lcol)]
        gathered = [share(mine[0])]
        dh, dg = grad_phase(1024, 1024, st, e1, tg, lcol, mtp_up, mtp_down, embed_table, mine[0])
        for i in range(1, len(PIECES)):
            mine.append(piece(i, dg if i == 1 else mine[-1]))
            gathered.append(share(mine[-1]))
            if i == 1:
                dg_all = share(dg)

        dsv, dpre, hid, dx, q_part = backward(S, BWD_ROWS, 1024, starts[-1] * TILE_V, TILE_V, AHEAD, dh, xs, w_in, w_in_t, w_out_t, nall, lse, tgt, embed_table, mine[-1])
        g_up = lax.dot_general(xs, dpre, (((0,), (0,)), ((), ())), preferred_element_type=F32)
        g_down = lax.dot_general(hid, dsv, (((0,), (0,)), ((), ())), preferred_element_type=F32)
        loss = (0.5 * jnp.sum(lall[:, 1, 0]) / N).reshape(1)

        lab_sorted, lab_perm = lax.sort((lab, lax.iota(jnp.int32, N)), num_keys=1)
        dg_rows = dg_all[jnp.pad(lab_perm, (0, WIN))]
        n_tile = pl.cdiv(V, TILE_V)
        lim = limits(tok, lab_sorted, TILE_V, n_tile)
        tokw = windows(tok, (1, 0, 0, 0))
        labw = windows(lab_sorted, (0, 1, 1, 1))
        ends = starts[1:] + [pl.cdiv(n_tile, SUB) * SUB]
        span = [(a // SUB, (b - a) // SUB) for a, b in zip(starts, ends)]
        early = [0, 1, len(PIECES)]
        stock = gathered + [q_part]
        full = sweep(TILE_V, [span[i] for i in early], [stock[i] for i in early], lim, tokw, dx, labw, dg_rows, V, None)
        for i in range(2, len(PIECES)):
            full = sweep(TILE_V, [span[i]], [stock[i]], lim, tokw, dx, labw, dg_rows, V, full)
        return loss, g_up[None], g_down[None], full

    in_specs = (P('dp'),) * 3 + (P(), P('stage'), P('stage'), P(), P())
    out_specs = (P('dp'), P(('dp', 'stage')), P(('dp', 'stage')), P('dp'))
    return jax.shard_map(per_device, mesh=mesh, in_specs=in_specs, out_specs=out_specs, check_vma=False)
```

time: 703 us -> 556 us (0.79)
  the two profiles are of different devices: /device:TPU:117 before, /device:TPU:116 now
where the time goes in v2:
time: 556 us; the launch traced here: 550 us
  Pallas kernels  470 us (85%)
  matrix products  26.7 us (5%)
  local copies, waits for them, and re-layouts  24 us (4%)
  between operations  16 us (3%)
  other arithmetic  12 us (2%)
    pallas_call x1, Pallas kernels, backward(): pl.pallas_call(functools.partial(bwd_kernel, S, C, tile, row0, pre), out_...  203 us
    pallas_call x2, Pallas kernels, sweep(): pl.pallas_call(functools.partial(sweep_kernel, tv, parts), out_shape=jax....  68.1 us
    pallas_call x1, Pallas kernels, forward(): pl.pallas_call(functools.partial(fwd_kernel, S, C, tile), out_shape=(jax....  56.4 us
    pallas_call x1, Pallas kernels, grad_phase(): pl.pallas_call(functools.partial(grad_kernel, TV, tile), out_shape=(jax.S...  52.5 us
    pallas_call x1, Pallas kernels, lse_phase(): pl.pallas_call(functools.partial(lse_kernel, S, TV, tile), out_shape=(jax...  47.7 us
    pallas_call x3, Pallas kernels, head_shard(): pl.pallas_call(shard_kernel, out_shape=jax.ShapeDtypeStruct((n_tile * tv,...  42.7 us
    dot_general x1, matrix products, per_device(): lax.dot_general(xs, dpre, (((0,), (0,)), ((), ())), preferred_element_typ...  15.3 us
    dot_general x1, matrix products, per_device(): lax.dot_general(hid, dsv, (((0,), (0,)), ((), ())), preferred_element_typ...  11.4 us
  transfers between devices with their start and end apart: 4, of which 0 were waited for; matrix products, arithmetic and copies ran while one was open for 8% of the time, Pallas kernels for 53%

profile of v2, /device:TPU:116, one launch (start us, length us, event | category | flops | bytes accessed | tf_op | source)
XLA Modules:
  0.0 550.2 jit_solution(6823930098266587150)
XLA Ops:
  7.2 0.1 all-gather.5.cloned.1.call-start
  7.3 0.7 copy.15
  8.0 0.7 copy.16
  8.7 0.7 copy.17
  9.4 5.1 sort.46
  14.5 0.0 copy-start
  14.5 0.0 copy-start.2
  14.5 0.1 dynamic_slice.13
  14.6 0.1 dynamic_slice.12
  14.7 0.1 dynamic_slice.11
  14.8 0.6 reshape.233.tgt_ref
  15.4 0.0 copy-done
  15.4 0.0 copy-done.2
  15.4 0.9 copy.14.tg_ref
  16.3 5.2 gather_fusion
  21.5 0.9 fusion.1
  22.4 56.4 %fwd_pipe.1 = (bf16[2048,512]{1,0:T(8,128)(2,1)}, bf16[256,512]{1,0:T(8,128)(2,1)}, bf16[4096,512]{1,0:T(8,128)(2,1)}, bf16[512,4096]{1,0:T(8,128)(2,1)}) custom-call(bf16[256,512]{1,0:T(8,128)(2,1)} %get-tuple-element.54.x_ref, bf16[512,4096]{1,0:T(8,128)(2,1)} %bitcast.55, bf16[4096,512]{1,0:T(8,128)(2,1)} %bitcast.54), custom_call_target="tpu_custom_call" | custom-call | flops 34359738368 | bytes 16777216 | tf_op jit(solution)/shard_map/fwd_pipe/pallas_call | solution.py:157
  78.8 47.7 %heads_lse.1 = (bf16[8,512,512]{2,1,0:T(8,128)(2,1)}, f32[8,8,512]{2,1,0:T(8,128)}, bf16[512,512]{1,0:T(8,128)(2,1)}, f32[512,128]{1,0:T(8,128)}) custom-call(bf16[256,512]{1,0:T(8,128)(2,1)} %get-tuple-element.30.h_ref, bf16[256,512]{1,0:T(8,128)(2,1)} %get-tuple-element.53.e1_ref, bf16[256,512]{1,0:T(8,128)(2,1)} %get-tuple-element.52.e2_ref, ...), custom_call_target="tpu_custom_call" | custom-call | flops 33688649728 | bytes 131596288 | tf_op jit(solution)/shard_map/heads_lse/pallas_call | solution.py:307
  126.5 1.5 slice.127
  128.0 14.2 %head_shard.3.after_ref = f32[1024,512]{1,0:T(8,128)} custom-call(s32[1]{0:T(128)} %bitcast.7.off_ref, bf16[32128,512]{1,0:T(8,128)(2,1)} %emb_ref.5, bf16[4096,512]{1,0:T(8,128)(2,1)} %bitcast.32, f32[4,1,1024]{2,1,0:T(1,128)} %bitcast.36, s32[4,1,1024]{2,1,0:T(1,128)} %reshape.233.tgt_ref, f32[512,128]{1,0:T(8,128)} %get-tuple-element.34.after_ref.lcol_ref), custom_call_target="tpu_custom_call" | custom-call | flops 17179869184 | bytes 4194304 | tf_op jit(solution)/shard_map/head_shard/pallas_call | solution.py:665
  142.2 52.5 %heads_grad.1 = (bf16[256,512]{1,0:T(8,128)(2,1)}, f32[256,512]{1,0:T(8,128)}) custom-call(bf16[512,512]{1,0:T(8,128)(2,1)} %get-tuple-element.33.st_ref, bf16[256,512]{1,0:T(8,128)(2,1)} %get-tuple-element.53.e1_ref, s32[512,1]{1,0:T(8,128)} %copy.14.tg_ref, f32[512,128]{1,0:T(8,128)} %get-tuple-element.34.after_ref.lcol_ref, bf16[512,4096]{1,0:T(8,128)(2,1)} %wi_ref.3, ...), custom_call_target="tpu_custom_call" | custom-call | flops 33688649728 | bytes 131596288 | tf_op jit(solution)/shard_map/heads_grad/pallas_call | solution.py:407
  194.7 0.1 all-gather.5.cloned.1.call-update
  194.7 0.1 all-gather.9.cloned.1.call-start
  194.8 0.7 all-gather.9.cloned.1.call-update
  195.6 0.1 all-gather.11.cloned.1.call-start
  195.6 19.6 %head_shard.4.after_ref = f32[1536,512]{1,0:T(8,128)} custom-call(s32[1]{0:T(128)} %bitcast.13.off_ref, bf16[32128,512]{1,0:T(8,128)(2,1)} %emb_ref.5, bf16[4096,512]{1,0:T(8,128)(2,1)} %bitcast.33, f32[4,1,1024]{2,1,0:T(1,128)} %bitcast.37, s32[4,1,1024]{2,1,0:T(1,128)} %reshape.233.tgt_ref, f32[256,512]{1,0:T(8,128)} %get-tuple-element.39.after_ref), custom_call_target="tpu_custom_call" | custom-call | flops 25769803776 | bytes 6291456 | tf_op jit(solution)/shard_map/head_shard/pallas_call | solution.py:665
  215.3 0.1 all-gather.11.cloned.1.call-update
  215.3 0.1 all-gather.7.cloned.1.call-start
  215.4 0.0 copy-start.1
  215.4 0.0 copy-start.3
  215.4 8.8 %head_shard.5.after_ref = f32[512,512]{1,0:T(8,128)} custom-call(s32[1]{0:T(128)} %bitcast.12.off_ref, bf16[32128,512]{1,0:T(8,128)(2,1)} %emb_ref.5, bf16[4096,512]{1,0:T(8,128)(2,1)} %bitcast.34, f32[4,1,1024]{2,1,0:T(1,128)} %bitcast.38, s32[4,1,1024]{2,1,0:T(1,128)} %reshape.233.tgt_ref, f32[1536,512]{1,0:T(8,128)} %head_shard.4.after_ref), custom_call_target="tpu_custom_call" | custom-call | flops 8589934592 | bytes 2097152 | tf_op jit(solution)/shard_map/head_shard/pallas_call | solution.py:665
  224.3 0.1 all-gather.7.cloned.1.call-update
  224.3 0.0 copy-done.1
  224.3 0.1 slice.132
  224.4 0.0 copy-done.3
  224.4 4.4 sort.47
  228.9 0.1 pad_slice_fusion.3
  228.9 0.1 slice.138
  229.0 0.1 slice.139
  229.1 0.1 pad_slice_fusion
  229.2 0.1 slice.145
  229.3 0.1 slice.136
  229.4 0.1 slice.134
  229.5 0.1 slice.143
  229.5 0.1 slice.141
  229.6 0.3 concatenate.49
  229.9 0.7 pad.20.labw_ref
  230.6 0.2 concatenate.48
  230.8 0.7 pad.18.tokw_ref
  231.4 1.4 slice_reduce_fusion
  233.5 0.3 convert_reduce_fusion.1
  233.7 0.1 maximum_bitcast_fusion
  233.8 0.6 pad_add_fusion.2.lim_ref
  234.4 203.0 %bwd_pipe.1 = (bf16[2048,512]{1,0:T(8,128)(2,1)}, bf16[2048,4096]{1,0:T(8,128)(2,1)}, bf16[2048,4096]{1,0:T(8,128)(2,1)}, bf16[2112,512]{1,0:T(8,128)(2,1)}, f32[7680,512]{1,0:T(8,128)}) custom-call(bf16[256,512]{1,0:T(8,128)(2,1)} %get-tuple-element.36.dh_ref, bf16[2048,512]{1,0:T(8,128)(2,1)} %get-tuple-element.32.xs_ref, bf16[512,4096]{1,0:T(8,128)(2,1)} %bitcast.56, ...), custom_call_target="tpu_custom_call" | custom-call | flops 34359738368 | bytes 67108864 | tf_op jit(solution)/shard_map/bwd_pipe/pallas_call | solution.py:613
  437.4 0.0 copy-start.4
  437.4 0.0 copy-start.5
  437.5 15.3 %convolution_bitcast_fusion.1 = f32[1,512,4096]{2,1,0:T(8,128)} fusion(bf16[2048,512]{1,0:T(8,128)(2,1)} %get-tuple-element.32.xs_ref, bf16[2048,4096]{1,0:T(8,128)(2,1)} %get-tuple-element.40), kind=kOutput, calls=%fused_computation.3 | convolution fusion | flops 8589934592 | bytes 27262976 | tf_op jit(solution)/shard_map/dot_general | solution.py:822
  452.8 0.0 copy-done.4
  452.8 0.0 copy-done.5
  452.8 11.4 %convolution_bitcast_fusion = f32[1,4096,512]{2,1,0:T(8,128)} fusion(bf16[2048,4096]{1,0:T(8,128)(2,1)S(1)} %copy-done.4, bf16[2048,512]{1,0:T(8,128)(2,1)S(1)} %copy-done.5), kind=kOutput, calls=%fused_computation.2 | convolution fusion | flops 8589934592 | bytes 27262976 | tf_op jit(solution)/shard_map/dot_general | solution.py:823
  464.1 0.0 all-gather.5.cloned.1.call-done
  464.1 10.0 %gather_fusion.1 = f32[2112,512]{1,0:T(8,128)} fusion(f32[2048,512]{1,0:T(8,128)} %all-gather.5.cloned.1.call-done, s32[3072]{0:T(1024)S(1)} %pad_clamp_fusion), kind=kCustom, calls=%fused_computation.1 | custom fusion | bytes 8659200 | tf_op jit(solution)/shard_map/gather | solution.py:827
  474.2 58.4 %sweep.2.refs_1_ = f32[32128,512]{1,0:T(8,128)} custom-call(s32[3,63]{1,0:T(4,128)} %pad_add_fusion.2.lim_ref, s32[129,256]{1,0:T(8,128)} %pad.18.tokw_ref, bf16[2112,512]{1,0:T(8,128)(2,1)} %get-tuple-element.44.dx_ref, s32[129,256]{1,0:T(8,128)} %pad.20.labw_ref, f32[2112,512]{1,0:T(8,128)} %gather_fusion.1, ...), custom_call_target="tpu_custom_call" | custom-call | flops 117440512 | bytes 117440512 | tf_op jit(solution)/shard_map/sweep/pallas_call | solution.py:734
  532.5 9.8 %sweep.3 = f32[32128,512]{1,0:T(8,128)} custom-call(s32[3,63]{1,0:T(4,128)} %pad_add_fusion.2.lim_ref, s32[129,256]{1,0:T(8,128)} %pad.18.tokw_ref, bf16[2112,512]{1,0:T(8,128)(2,1)} %get-tuple-element.44.dx_ref, s32[129,256]{1,0:T(8,128)} %pad.20.labw_ref, f32[2112,512]{1,0:T(8,128)} %gather_fusion.1, ...), custom_call_target="tpu_custom_call", output_to_operand_aliasing={{}: (6, {})} | custom-call | flops 16777216 | bytes 16777216 | tf_op jit(solution)/shard_map/sweep/pallas_call | solution.py:734
  (14 shorter events, 0.1 us)
Async XLA Ops:
  7.2 457.0 %all-gather.5.cloned.1.call-start = ((), (), s32[]{:S(2)}) async-start(), calls=%async_computation | async-start | bytes 4718592 | tf_op jit(solution)/shard_map/all_gather | solution.py:810
  14.5 0.9 copy-start
  14.5 0.9 copy-start.2
  194.7 279.4 %all-gather.9.cloned.1.call-start = ((), (), s32[]{:S(2)}) async-start(), calls=%async_computation.2 | async-start | bytes 18874368 | tf_op jit(solution)/shard_map/all_gather | solution.py:810
  195.6 278.6 %all-gather.11.cloned.1.call-start = ((), (), s32[]{:S(2)}) async-start(), calls=%async_computation.3 | async-start | bytes 28311552 | tf_op jit(solution)/shard_map/all_gather | solution.py:810
  215.3 317.2 %all-gather.7.cloned.1.call-start = ((), (), s32[]{:S(2)}) async-start(), calls=%async_computation.1 | async-start | bytes 9437184 | tf_op jit(solution)/shard_map/all_gather | solution.py:810
  215.4 8.9 %copy-start.1 = (s32[2048]{0:T(1024)S(1)}, s32[2048]{0:T(1024)}, u32[]{:S(2)}) copy-start(s32[2048]{0:T(1024)} %copy-done) | copy-start | bytes 24580
  215.4 9.0 %copy-start.3 = (s32[2048]{0:T(1024)S(1)}, s32[2048]{0:T(1024)}, u32[]{:S(2)}) copy-start(s32[2048]{0:T(1024)} %copy-done.2) | copy-start | bytes 24580
  437.4 15.3 %copy-start.4 = (bf16[2048,4096]{1,0:T(8,128)(2,1)S(1)}, bf16[2048,4096]{1,0:T(8,128)(2,1)}, u32[]{:S(2)}) copy-start(bf16[2048,4096]{1,0:T(8,128)(2,1)} %get-tuple-element.41) | copy-start | bytes 50331652
  437.4 15.3 %copy-start.5 = (bf16[2048,512]{1,0:T(8,128)(2,1)S(1)}, bf16[2048,512]{1,0:T(8,128)(2,1)}, u32[]{:S(2)}) copy-start(bf16[2048,512]{1,0:T(8,128)(2,1)} %get-tuple-element.42) | copy-start | bytes 6291460
Sparse Core Ops, SparseCore 0:
  194.9 28.5 all-gather.4
  225.0 98.9 all-gather.8
  326.2 137.3 all-gather.10
  465.0 45.7 all-gather.6

commit v3 on v2

--- a/solution.py
+++ b/solution.py
@@ -565,7 +565,7 @@
 
         for cp in out_copies(c):
             cp.start()
-        units(ahead + c, ahead + c + 1)
+        units(ahead + c * PER_CHUNK, ahead + (c + 1) * PER_CHUNK)
         return carry
 
     lax.fori_loop(0, n_chunk, step, 0)
@@ -579,7 +579,7 @@
         for j in range(per):
             rcopy(dh_ref.at[rows(j, C)], ds_ref.at[rows(me * per + j, C)], own_sem.at[j], recv_sem.at[me * per + j], last).wait_send()
 
-    done = jnp.minimum(ahead + n_chunk, n_unit)
+    done = jnp.minimum(ahead + n_chunk * PER_CHUNK, n_unit)
     left = (n_unit - done + n_chunk - 1) // n_chunk
 
     def drain(c, carry):
@@ -770,8 +770,10 @@
 WIN = 64
 STEP = 16
 AHEAD = 4
-SUB = 2
-PIECES = (2, 3, 1)
+PER_CHUNK = 1
+SUB = 4
+HALF_V = TILE_V // 2
+PIECES = (4, 6, 3)
 FWD_ROWS = 128
 BWD_ROWS = 128
 
@@ -800,11 +802,13 @@
         lse = lall[:, 0, :].reshape(2 * N // TOKENS, 1, TOKENS)
         tgt = jnp.stack([lab.reshape(S, R), lab2.reshape(S, R)], axis=1).reshape(2 * N // TOKENS, 1, TOKENS)
 
-        starts = [S * sum(PIECES[:i]) for i in range(len(PIECES) + 1)]
+        starts = [S * sum(PIECES[:i]) * HALF_V // TILE_V for i in range(len(PIECES) + 1)]
 
         def piece(i, after):
-            off = (starts[i] + me * PIECES[i]).reshape(1)
-            return head_shard(TILE_V, PIECES[i], off, embed_table, nall, lse, tgt, after)
+            tv = HALF_V if PIECES[i] % 2 else TILE_V
+            n = PIECES[i] * HALF_V // tv
+            off = (starts[i] * TILE_V // tv + me * n).reshape(1)
+            return head_shard(tv, n, off, embed_table, nall, lse, tgt, after)
 
         def share(v):
             return lax.all_gather(v, AXIS, axis=0, tiled=True)

time: 556 us -> 556 us (level)
  the two profiles are of different devices: /device:TPU:116 before, /device:TPU:112 now
where the time goes in v3:
time: 556 us; the launch traced here: 551 us
  Pallas kernels  410 us (74%)
  waiting for transfers between devices  61 us (11%)
  matrix products  26.8 us (5%)
  local copies, waits for them, and re-layouts  24.1 us (4%)
  between operations  16 us (3%)
  other arithmetic  11.9 us (2%)
    pallas_call x1, Pallas kernels, backward(): pl.pallas_call(functools.partial(bwd_kernel, S, C, tile, row0, pre), out_...  145 us
    pallas_call x1, Pallas kernels, lse_phase(): pl.pallas_call(functools.partial(lse_kernel, S, TV, tile), out_shape=(jax...  61 us
    pallas_call x2, Pallas kernels, sweep(): pl.pallas_call(functools.partial(sweep_kernel, tv, parts), out_shape=jax....  60.1 us
    all_gather x4, waiting for transfers between devices, share(): return lax.all_gather(v, AXIS, axis=0, tiled=True)  60.1 us
    pallas_call x1, Pallas kernels, grad_phase(): pl.pallas_call(functools.partial(grad_kernel, TV, tile), out_shape=(jax.S...  52.5 us
    pallas_call x3, Pallas kernels, head_shard(): pl.pallas_call(shard_kernel, out_shape=jax.ShapeDtypeStruct((n_tile * tv,...  46.5 us
    pallas_call x1, Pallas kernels, forward(): pl.pallas_call(functools.partial(fwd_kernel, S, C, tile), out_shape=(jax....  45.6 us
    dot_general x1, matrix products, per_device(): lax.dot_general(xs, dpre, (((0,), (0,)), ((), ())), preferred_element_typ...  15.4 us
  transfers between devices with their start and end apart: 4, of which 2 were waited for; matrix products, arithmetic and copies ran while one was open for 8% of the time, Pallas kernels for 41%

profile of v3, /device:TPU:112, one launch (start us, length us, event | category | flops | bytes accessed | tf_op | source)
XLA Modules:
  0.0 550.6 jit_solution(7754431387599499024)
XLA Ops:
  7.2 0.1 all-gather.5.cloned.1.call-start
  7.3 0.7 copy.15
  8.0 0.7 copy.16
  8.7 0.7 copy.17
  9.4 5.1 sort.46
  14.5 0.0 copy-start
  14.5 0.1 dynamic_slice.13
  14.6 0.1 dynamic_slice.12
  14.7 0.1 dynamic_slice.11
  14.8 0.6 reshape.233.tgt_ref
  15.4 0.0 copy-done
  15.4 0.0 copy-done.2
  15.4 0.9 copy.14.tg_ref
  16.3 5.3 gather_fusion
  21.6 0.9 fusion.1
  22.5 45.6 %fwd_pipe.1 = (bf16[2048,512]{1,0:T(8,128)(2,1)}, bf16[256,512]{1,0:T(8,128)(2,1)}, bf16[4096,512]{1,0:T(8,128)(2,1)}, bf16[512,4096]{1,0:T(8,128)(2,1)}) custom-call(bf16[256,512]{1,0:T(8,128)(2,1)} %get-tuple-element.54.x_ref, bf16[512,4096]{1,0:T(8,128)(2,1)} %bitcast.51, bf16[4096,512]{1,0:T(8,128)(2,1)} %bitcast.50), custom_call_target="tpu_custom_call" | custom-call | flops 34359738368 | bytes 16777216 | tf_op jit(solution)/shard_map/fwd_pipe/pallas_call | solution.py:157
  68.1 61.0 %heads_lse.1 = (bf16[8,512,512]{2,1,0:T(8,128)(2,1)}, f32[8,8,512]{2,1,0:T(8,128)}, bf16[512,512]{1,0:T(8,128)(2,1)}, f32[512,128]{1,0:T(8,128)}) custom-call(bf16[256,512]{1,0:T(8,128)(2,1)} %get-tuple-element.30.h_ref, bf16[256,512]{1,0:T(8,128)(2,1)} %get-tuple-element.53.e1_ref, bf16[256,512]{1,0:T(8,128)(2,1)} %get-tuple-element.52.e2_ref, ...), custom_call_target="tpu_custom_call" | custom-call | flops 33688649728 | bytes 131596288 | tf_op jit(solution)/shard_map/heads_lse/pallas_call | solution.py:307
  129.1 1.5 slice.127
  130.6 14.2 %head_shard.3.after_ref = f32[1024,512]{1,0:T(8,128)} custom-call(s32[1]{0:T(128)} %bitcast.7.off_ref, bf16[32128,512]{1,0:T(8,128)(2,1)} %emb_ref.5, bf16[4096,512]{1,0:T(8,128)(2,1)} %bitcast.53, f32[4,1,1024]{2,1,0:T(1,128)} %bitcast.36, s32[4,1,1024]{2,1,0:T(1,128)} %reshape.233.tgt_ref, f32[512,128]{1,0:T(8,128)} %get-tuple-element.34.after_ref.lcol_ref), custom_call_target="tpu_custom_call" | custom-call | flops 17179869184 | bytes 4194304 | tf_op jit(solution)/shard_map/head_shard/pallas_call | solution.py:665
  144.8 52.5 %heads_grad.1 = (bf16[256,512]{1,0:T(8,128)(2,1)}, f32[256,512]{1,0:T(8,128)}) custom-call(bf16[512,512]{1,0:T(8,128)(2,1)} %get-tuple-element.33.st_ref, bf16[256,512]{1,0:T(8,128)(2,1)} %get-tuple-element.53.e1_ref, s32[512,1]{1,0:T(8,128)} %copy.14.tg_ref, f32[512,128]{1,0:T(8,128)} %get-tuple-element.34.after_ref.lcol_ref, bf16[512,4096]{1,0:T(8,128)(2,1)} %wi_ref.3, ...), custom_call_target="tpu_custom_call" | custom-call | flops 33688649728 | bytes 131596288 | tf_op jit(solution)/shard_map/heads_grad/pallas_call | solution.py:407
  197.2 0.1 all-gather.5.cloned.1.call-update
  197.3 0.1 all-gather.9.cloned.1.call-start
  197.4 0.7 all-gather.9.cloned.1.call-update
  198.1 0.1 all-gather.11.cloned.1.call-start
  198.2 19.6 %head_shard.4.after_ref = f32[1536,512]{1,0:T(8,128)} custom-call(s32[1]{0:T(128)} %bitcast.13.off_ref, bf16[32128,512]{1,0:T(8,128)(2,1)} %emb_ref.5, bf16[4096,512]{1,0:T(8,128)(2,1)} %bitcast.54, f32[4,1,1024]{2,1,0:T(1,128)} %bitcast.37, s32[4,1,1024]{2,1,0:T(1,128)} %reshape.233.tgt_ref, f32[256,512]{1,0:T(8,128)} %get-tuple-element.39.after_ref), custom_call_target="tpu_custom_call" | custom-call | flops 25769803776 | bytes 6291456 | tf_op jit(solution)/shard_map/head_shard/pallas_call | solution.py:665
  217.8 0.1 all-gather.11.cloned.1.call-update
  217.9 0.1 all-gather.7.cloned.1.call-start
  218.0 0.0 copy-start.1
  218.0 0.0 copy-start.3
  218.0 12.7 %head_shard.5.after_ref = f32[768,512]{1,0:T(8,128)} custom-call(s32[1]{0:T(128)} %bitcast.12.off_ref, bf16[32128,512]{1,0:T(8,128)(2,1)} %emb_ref.5, bf16[4096,512]{1,0:T(8,128)(2,1)} %bitcast.55, f32[4,1,1024]{2,1,0:T(1,128)} %bitcast.38, s32[4,1,1024]{2,1,0:T(1,128)} %reshape.233.tgt_ref, f32[1536,512]{1,0:T(8,128)} %head_shard.4.after_ref), custom_call_target="tpu_custom_call" | custom-call | flops 12884901888 | bytes 3145728 | tf_op jit(solution)/shard_map/head_shard/pallas_call | solution.py:665
  230.7 0.1 all-gather.7.cloned.1.call-update
  230.7 0.0 copy-done.1
  230.7 0.1 slice.132
  230.8 0.0 copy-done.3
  230.9 4.4 sort.47
  235.3 0.1 pad_slice_fusion.3
  235.4 0.1 slice.138
  235.5 0.1 slice.139
  235.5 0.1 pad_slice_fusion
  235.6 0.1 slice.145
  235.7 0.1 slice.136
  235.8 0.1 slice.134
  235.9 0.1 slice.143
  235.9 0.1 slice.141
  236.0 0.3 concatenate.49
  236.3 0.7 pad.20.labw_ref
  237.0 0.2 concatenate.48
  237.2 0.7 pad.18.tokw_ref
  237.8 1.4 slice_reduce_fusion
  239.9 0.3 convert_reduce_fusion.1
  240.2 0.1 maximum_bitcast_fusion
  240.2 0.6 pad_add_fusion.2.lim_ref
  240.8 144.8 %bwd_pipe.1 = (bf16[2048,512]{1,0:T(8,128)(2,1)}, bf16[2048,4096]{1,0:T(8,128)(2,1)}, bf16[2048,4096]{1,0:T(8,128)(2,1)}, bf16[2112,512]{1,0:T(8,128)(2,1)}, f32[5632,512]{1,0:T(8,128)}) custom-call(bf16[256,512]{1,0:T(8,128)(2,1)} %get-tuple-element.36.dh_ref, bf16[2048,512]{1,0:T(8,128)(2,1)} %get-tuple-element.32.xs_ref, bf16[512,4096]{1,0:T(8,128)(2,1)} %bitcast.52, ...), custom_call_target="tpu_custom_call" | custom-call | flops 34359738368 | bytes 67108864 | tf_op jit(solution)/shard_map/bwd_pipe/pallas_call | solution.py:613
  385.7 0.0 copy-start.4
  385.7 0.0 copy-start.5
  385.7 15.4 %convolution_bitcast_fusion.1 = f32[1,512,4096]{2,1,0:T(8,128)} fusion(bf16[2048,512]{1,0:T(8,128)(2,1)} %get-tuple-element.32.xs_ref, bf16[2048,4096]{1,0:T(8,128)(2,1)} %get-tuple-element.40), kind=kOutput, calls=%fused_computation.3 | convolution fusion | flops 8589934592 | bytes 27262976 | tf_op jit(solution)/shard_map/dot_general | solution.py:826
  401.1 0.0 copy-done.4
  401.1 0.0 copy-done.5
  401.1 11.4 %convolution_bitcast_fusion = f32[1,4096,512]{2,1,0:T(8,128)} fusion(bf16[2048,4096]{1,0:T(8,128)(2,1)S(1)} %copy-done.4, bf16[2048,512]{1,0:T(8,128)(2,1)S(1)} %copy-done.5), kind=kOutput, calls=%fused_computation.2 | convolution fusion | flops 8589934592 | bytes 27262976 | tf_op jit(solution)/shard_map/dot_general | solution.py:827
  412.5 10.1 %gather_fusion.1 = f32[2112,512]{1,0:T(8,128)} fusion(f32[2048,512]{1,0:T(8,128)} %all-gather.5.cloned.1.call-done, s32[3072]{0:T(1024)S(1)} %pad_clamp_fusion), kind=kCustom, calls=%fused_computation.1 | custom fusion | bytes 8659200 | tf_op jit(solution)/shard_map/gather | solution.py:831
  422.6 31.1 %all-gather.11.cloned.1.call-done.refs_1_ = f32[12288,512]{1,0:T(8,128)} async-done(((f32[1536,512]{1,0:T(8,128)}), f32[12288,512]{1,0:T(8,128)}) %all-gather.11.cloned.1.call-update) | async-done | bytes 25165840 | tf_op jit(solution)/shard_map/all_gather | solution.py:814
  453.6 47.1 %sweep.2.refs_1_ = f32[32128,512]{1,0:T(8,128)} custom-call(s32[3,63]{1,0:T(4,128)} %pad_add_fusion.2.lim_ref, s32[129,256]{1,0:T(8,128)} %pad.18.tokw_ref, bf16[2112,512]{1,0:T(8,128)(2,1)} %get-tuple-element.44.dx_ref, s32[129,256]{1,0:T(8,128)} %pad.20.labw_ref, f32[2112,512]{1,0:T(8,128)} %gather_fusion.1, ...), custom_call_target="tpu_custom_call" | custom-call | flops 109051904 | bytes 109051904 | tf_op jit(solution)/shard_map/sweep/pallas_call | solution.py:734
  500.7 29.0 %all-gather.7.cloned.1.call-done.refs_0_ = f32[6144,512]{1,0:T(8,128)} async-done(((f32[768,512]{1,0:T(8,128)}), f32[6144,512]{1,0:T(8,128)}) %all-gather.7.cloned.1.call-update) | async-done | bytes 12582928 | tf_op jit(solution)/shard_map/all_gather | solution.py:814
  529.7 13.0 %sweep.3 = f32[32128,512]{1,0:T(8,128)} custom-call(s32[3,63]{1,0:T(4,128)} %pad_add_fusion.2.lim_ref, s32[129,256]{1,0:T(8,128)} %pad.18.tokw_ref, bf16[2112,512]{1,0:T(8,128)(2,1)} %get-tuple-element.44.dx_ref, s32[129,256]{1,0:T(8,128)} %pad.20.labw_ref, f32[2112,512]{1,0:T(8,128)} %gather_fusion.1, ...), custom_call_target="tpu_custom_call", output_to_operand_aliasing={{}: (6, {})} | custom-call | flops 25165824 | bytes 25165824 | tf_op jit(solution)/shard_map/sweep/pallas_call | solution.py:734
  (14 shorter events, 0.1 us)
Async XLA Ops:
  7.2 405.3 %all-gather.5.cloned.1.call-start = ((), (), s32[]{:S(2)}) async-start(), calls=%async_computation | async-start | bytes 4718592 | tf_op jit(solution)/shard_map/all_gather | solution.py:814
  14.5 0.9 copy-start
  14.5 0.9 copy-start.2
  197.3 225.3 %all-gather.9.cloned.1.call-start = ((), (), s32[]{:S(2)}) async-start(), calls=%async_computation.2 | async-start | bytes 18874368 | tf_op jit(solution)/shard_map/all_gather | solution.py:814
  198.1 255.5 %all-gather.11.cloned.1.call-start = ((), (), s32[]{:S(2)}) async-start(), calls=%async_computation.3 | async-start | bytes 28311552 | tf_op jit(solution)/shard_map/all_gather | solution.py:814
  217.9 311.8 %all-gather.7.cloned.1.call-start = ((), (), s32[]{:S(2)}) async-start(), calls=%async_computation.1 | async-start | bytes 14155776 | tf_op jit(solution)/shard_map/all_gather | solution.py:814
  218.0 12.8 %copy-start.1 = (s32[2048]{0:T(1024)S(1)}, s32[2048]{0:T(1024)}, u32[]{:S(2)}) copy-start(s32[2048]{0:T(1024)} %copy-done) | copy-start | bytes 24580
  218.0 12.9 %copy-start.3 = (s32[2048]{0:T(1024)S(1)}, s32[2048]{0:T(1024)}, u32[]{:S(2)}) copy-start(s32[2048]{0:T(1024)} %copy-done.2) | copy-start | bytes 24580
  385.7 15.5 %copy-start.4 = (bf16[2048,4096]{1,0:T(8,128)(2,1)S(1)}, bf16[2048,4096]{1,0:T(8,128)(2,1)}, u32[]{:S(2)}) copy-start(bf16[2048,4096]{1,0:T(8,128)(2,1)} %get-tuple-element.41) | copy-start | bytes 50331652
  385.7 15.5 %copy-start.5 = (bf16[2048,512]{1,0:T(8,128)(2,1)S(1)}, bf16[2048,512]{1,0:T(8,128)(2,1)}, u32[]{:S(2)}) copy-start(bf16[2048,512]{1,0:T(8,128)(2,1)} %get-tuple-element.42) | copy-start | bytes 6291460
Sparse Core Ops, SparseCore 0:
  197.4 28.2 all-gather.4
  227.4 92.1 all-gather.8
  321.7 131.8 all-gather.10
  455.1 74.6 all-gather.6
